TPU v7x, 32 devices: a whole 2x2x4 slice. The times are simulated.
32 devices in a mesh: row: 4 (over x, core), col: 8 (over z, y).
Axes of the slice: x: 2, y: 2, z: 4, core: 2. Of those that a mesh axis runs over, the one named last changes fastest.
Arguments:
- ancestor_inv: bfloat16 [32, 32, 256, 256], P('row', 'col'), may hold values from -0.29882812 to 0.29882812
- lower_panel: bfloat16 [8, 16, 256, 256], P('row', 'col'), may hold values from -0.59765625 to 0.59765625
- upper_panel: bfloat16 [8, 16, 256, 256], P('col', 'row'), may hold values from -0.59765625 to 0.59765625
- pivot_inv: float32 [8, 256, 256], P('col'), may hold values from -6 to 6
- members: int32 [8, 16], replicated, may hold values from -1 to 31, as said below
Outputs:
- lower_inv: bfloat16 [8, 16, 256, 256], P('col', 'row')
- upper_inv: bfloat16 [8, 16, 256, 256], P('row', 'col')
- diag_inv: float32 [8, 256, 256], P('col')
Inputs may be any that keep to these rules, and one draw needn't show every extreme that they name: `members`: slot s belongs to group g = s // 2; a used slot names an ancestor block of that group, from g * 4 to (g + 1) * 4 - 1. In each group of each supernode the used slots come first, name distinct blocks, and number 1 to 2; every group has 2 used slots for some supernode. Empty slots hold -1.
All inputs are finite; a program needn't handle non-finite values.
Results may differ from a plain program's by a relative error of at most 0.013.
Values may be sent and summed in bfloat16 or wider, within the bound.
A program may use at most 128 MiB of HBM per device.

v0:
```python
import functools

import jax
import jax.numpy as jnp
from jax import lax
from jax.experimental import pallas as pl
from jax.experimental.pallas import tpu as pltpu
from jax.sharding import PartitionSpec as P

NY = 2
CORES = 2
BF = jnp.bfloat16
F32 = jnp.float32


def kernel(
    n_row, n_col, nq, hp,
    mem, anc, low, upp, piv,
    low_out, upp_out, diag_out,
    a, lbuf, ubuf, pl_buf, yr, zr, pu, ur, ds, dr, acc, dacc,
    loc, l_s, l_rel, l_r, uy_s, uy_r, uz_s, uz_r, ry_s, ry_r, rz_s, rz_r, pu_s, pu_r, d_s, d_r,
):
    row = lax.axis_index("row")
    col = lax.axis_index("col")
    nz = n_col // NY
    nx = n_row // CORES
    x, core = row // CORES, row % CORES
    z, y = col // NY, col % NY
    yp = z * NY + (1 - y)
    rb, cb = anc.shape[0], anc.shape[1]
    kr, cs = low.shape[0], low.shape[1]
    rs = upp.shape[1]
    ny_blocks = rs - nq
    hb = rs // hp
    partner = x * CORES + (1 - core)

    def remote(src, dst, ss, rsem, **where):
        return pltpu.make_async_remote_copy(
            src_ref=src, dst_ref=dst, send_sem=ss, recv_sem=rsem, device_id=where
        )

    ca = pltpu.make_async_copy(anc, a, loc.at[0])
    cl = pltpu.make_async_copy(low, lbuf.at[pl.ds(row * kr, kr)], loc.at[1])
    cu = pltpu.make_async_copy(upp.at[0], ubuf.at[col], loc.at[2])
    cl.start()
    cu.start()
    ca.start()

    bar = pltpu.get_barrier_semaphore()
    for dx in range(1, n_row):
        pl.semaphore_signal(bar, inc=1, device_id={"row": (row + dx) % n_row})
    pl.semaphore_signal(bar, inc=1, device_id={"col": yp})

    @pl.when(z > 0)
    def _():
        pl.semaphore_signal(bar, inc=1, device_id={"col": col - NY})

    @pl.when(z < nz - 1)
    def _():
        pl.semaphore_signal(bar, inc=1, device_id={"col": col + NY})

    peers = n_row + jnp.where(z > 0, 1, 0) + jnp.where(z < nz - 1, 1, 0)
    pl.semaphore_wait(bar, peers)

    def l_own(r2):
        return remote(low, lbuf.at[pl.ds(row * kr, kr)], l_s.at[r2], l_r.at[row], row=r2)

    def l_recv(r2):
        blk = lbuf.at[pl.ds(r2 * kr, kr)]
        return remote(blk, blk, l_rel.at[r2], l_r.at[r2], row=partner)

    def uy_own(kind):
        part = pl.ds(0, ny_blocks) if kind else pl.ds(ny_blocks, nq)
        return remote(
            upp.at[0, part], ubuf.at[col, part], uy_s.at[nz if kind == 0 else z],
            uy_r.at[nz if kind == 0 else z], col=yp,
        )

    def uy_got(kind, zs):
        part = pl.ds(0, ny_blocks) if kind else pl.ds(ny_blocks, nq)
        blk = ubuf.at[zs * NY + (1 - y), part]
        return remote(blk, blk, uy_s.at[zs], uy_r.at[nz if kind == 0 else zs], col=yp)

    def uy_pass(zs):
        blk = ubuf.at[zs * NY + y, pl.ds(0, ny_blocks)]
        return remote(blk, blk, uy_s.at[zs], uy_r.at[zs], col=yp)

    def uz(zs, kind, up):
        if kind == 0:
            blk = ubuf.at[zs * NY + y]
        else:
            blk = ubuf.at[zs * NY + (1 - y), pl.ds(ny_blocks, nq)]
        to = col + NY if up else col - NY
        return remote(blk, blk, uz_s.at[zs, int(up), kind], uz_r.at[zs, kind], col=to)

    def uz_own(up):
        to = col + NY if up else col - NY
        return remote(upp.at[0], ubuf.at[col], uz_s.at[z, int(up), 0], uz_r.at[z, 0], col=to)

    def ry(zd, h):
        part = pl.ds(h * hb, hb)
        return remote(
            pl_buf.at[zd * NY + (1 - y), part], yr.at[zd, part], ry_s.at[zd, h], ry_r.at[zd, h],
            col=yp,
        )

    def rz(zd, h, up):
        part = pl.ds(h * hb, hb)
        slot = zd + 1 if up else zd
        to = col + NY if up else col - NY
        return remote(
            pl_buf.at[zd * NY + y, part], zr.at[slot, part], rz_s.at[zd, h], rz_r.at[slot, h],
            col=to,
        )

    def pu_copy(k):
        return remote(pu.at[k], ur.at[row, k % kr], pu_s.at[k], pu_r.at[row, k % kr], row=k // kr)

    def pu_got(r2, p):
        return remote(pu.at[0], ur.at[r2, p], pu_s.at[0], pu_r.at[r2, p], row=r2)

    def d_copy(r2):
        return remote(ds, dr.at[row], d_s.at[r2], d_r.at[row], row=r2)

    def d_got(r2):
        return remote(ds, dr.at[r2], d_s.at[r2], d_r.at[r2], row=r2)

    def d_relay(x2):
        r2 = x2 * CORES + core
        blk = dr.at[r2]
        return remote(blk, blk, d_s.at[x2 * CORES + 1 - core], d_r.at[r2], row=partner)

    def each_dir(fn):
        @pl.when(z > 0)
        def _():
            fn(False)

        @pl.when(z < nz - 1)
        def _():
            fn(True)

    def row_member(k, i):
        m = mem[k, row * rs + i]
        return m >= 0, jnp.clip(m - row * rb, 0, rb - 1)

    def col_member(k, j):
        m = mem[k, col * cs + j]
        return m >= 0, jnp.clip(m - col * cb, 0, cb - 1)

    zero = jnp.zeros((), BF)

    def lower_part(k):
        cols = [col_member(k, j) for j in range(cs)]
        panels = [jnp.where(cols[j][0], lbuf[k, j], zero) for j in range(cs)]

        def one(i, _):
            ok, ri = row_member(k, i)
            tot = None
            for j in range(cs):
                t = jnp.dot(a[ri, cols[j][1]], panels[j], preferred_element_type=F32)
                tot = t if tot is None else tot + t
            pl_buf[k, i] = jnp.where(ok, tot, 0.0).astype(BF)
            return 0

        lax.fori_loop(0, rs, one, 0)

    def upper_part(k):
        rows = [row_member(k, i) for i in range(rs)]

        def one(j, _):
            ok, cj = col_member(k, j)
            tot = None
            for i in range(rs):
                t = jnp.dot(
                    jnp.where(rows[i][0], ubuf[k, i], zero), a[rows[i][1], cj],
                    preferred_element_type=F32,
                )
                tot = t if tot is None else tot + t
            pu[k, j] = jnp.where(ok, tot, 0.0).astype(BF)
            return 0

        lax.fori_loop(0, cs, one, 0)

        @pl.when(k // kr != row)
        def _():
            pu_copy(k).start()

    def lower_group(r2):
        def one(p, _):
            k = r2 * kr + (p + 1 - y) % NY
            lower_part(k)

            @pl.when(k % NY != y)
            def _():
                for h in range(hp):
                    ry(k // NY, h).start()

            return 0

        lax.fori_loop(0, kr, one, 0)

    def target(t):
        x2 = (x + t // CORES) % nx
        q = t % CORES
        return x2 * CORES + jnp.where(2 * x2 >= nx, CORES - 1 - q, q)

    def both_groups(x2):
        def one(q, _):
            lower_group(x2 * CORES + jnp.where(2 * x2 >= nx, CORES - 1 - q, q))
            return 0

        lax.fori_loop(0, CORES, one, 0)

    l_own(partner).start()
    for dx in range(1, nx):
        l_own(((x + dx) % nx) * CORES + core).start()
    uy_own(0).start()
    each_dir(lambda up: uz_own(up).start())

    ca.wait()
    cl.wait()
    l_recv(partner).wait_recv()
    both_groups(x)

    uy_got(0, z).wait_recv()
    each_dir(lambda up: uz(z, 1, up).start())
    cu.wait()
    upper_part(col)

    def others(fn):
        for dx in range(1, nx):
            fn((x + dx) % nx)

    def relay(x2):
        l_recv(x2 * CORES + core).wait_recv()
        l_recv(x2 * CORES + core).start()

    others(relay)

    def by_side(d, fn):
        @pl.when(z - d >= 0)
        def _():
            fn(z - d, True)

        @pl.when(z + d <= nz - 1)
        def _():
            fn(z + d, False)

    def take(zs, up):
        for kind in range(2):
            uz(zs, kind, up).wait_recv()

            @pl.when((z < nz - 1) if up else (z > 0))
            def _():
                uz(zs, kind, up).start()

    by_side(1, take)

    def late(x2):
        l_recv(x2 * CORES + 1 - core).wait_recv()
        both_groups(x2)

    others(late)
    uy_own(1).start()
    by_side(1, lambda zs, up: uy_pass(zs).start())

    def near(d):
        def one(s, _):
            zs = z + (2 * s - 1) * d

            @pl.when(jnp.logical_and(zs >= 0, zs < nz))
            def _():
                upper_part(zs * NY + y)

            return 0

        lax.fori_loop(0, 2, one, 0)

    def far(d):
        def one(s, _):
            zs = z + (2 * s - 1) * d

            @pl.when(jnp.logical_and(zs >= 0, zs < nz))
            def _():
                uy_got(1, zs).wait_recv()
                upper_part(zs * NY + (1 - y))

            return 0

        lax.fori_loop(0, 2, one, 0)

    def band_sum(zd, t):
        k = zd * NY + y

        def go(up):
            def piece(h, _):
                part = pl.ds(h * hb, hb)
                ry(zd, h).wait_recv()

                @pl.when((z > 0) if up else (z < nz - 1))
                def _():
                    rz(zd, h, up).wait_recv()
                    slot = zd + 1 if up else zd
                    pl_buf[k, part] = (
                        pl_buf[k, part].astype(F32) + yr[zd, part].astype(F32)
                        + zr[slot, part].astype(F32)
                    ).astype(BF)

                @pl.when((z == 0) if up else (z == nz - 1))
                def _():
                    pl_buf[k, part] = (
                        pl_buf[k, part].astype(F32) + yr[zd, part].astype(F32)
                    ).astype(BF)

                rz(zd, h, up).start()
                return 0

            lax.fori_loop(0, hp, piece, 0)

        @pl.when(zd > z)
        def _():
            go(True)

        @pl.when(zd < z)
        def _():
            go(False)

    def chain(t):
        band_sum(target(t), t)

    near(1)
    edge = jnp.logical_or(z == 0, z == nz - 1)

    def take_pass(d):
        by_side(d, take)
        by_side(d, lambda zs, up: uy_pass(zs).start())
        near(d)

    def chains(t, _):
        chain(t)
        return 0

    @pl.when(edge)
    def _():
        lax.fori_loop(0, CORES, chains, 0)

    @pl.when(jnp.logical_not(edge))
    def _():
        def one(d, _):
            take_pass(d)
            return 0

        lax.fori_loop(2, nz - 1, one, 0)
        lax.fori_loop(0, CORES, chains, 0)

    @pl.when(edge)
    def _():
        def one(d, _):
            take_pass(d)
            chain(CORES + d - 2)
            return 0

        lax.fori_loop(2, nz, one, 0)

    @pl.when(jnp.logical_not(edge))
    def _():
        lax.fori_loop(CORES, nz, chains, 0)

    uy_got(1, z).wait_recv()
    upper_part(yp)
    far(1)

    def final(h, _):
        part = pl.ds(h * hb, hb)
        ry(z, h).wait_recv()
        acc[part] = pl_buf[col, part].astype(F32) + yr[z, part].astype(F32)

        @pl.when(z > 0)
        def _():
            rz(z, h, True).wait_recv()
            acc[part] = acc[part] + zr[z + 1, part].astype(F32)

        @pl.when(z < nz - 1)
        def _():
            rz(z, h, False).wait_recv()
            acc[part] = acc[part] + zr[z, part].astype(F32)

        low_out[0, part] = (-acc[part]).astype(BF)
        return 0

    lax.fori_loop(0, hp, final, 0)
    tot = None
    for i in range(rs):
        t = jnp.dot(
            jnp.where(row_member(col, i)[0], ubuf[col, i], zero), low_out[0, i],
            preferred_element_type=F32,
        )
        tot = t if tot is None else tot + t
    dacc[...] = tot
    ds[...] = tot.astype(BF)
    others(lambda x2: d_copy(x2 * CORES + core).start())
    d_copy(partner).start()

    lax.fori_loop(2, nz, lambda d, _: (far(d), 0)[1], 0)

    def d_pass(x2):
        d_got(x2 * CORES + core).wait_recv()
        d_relay(x2).start()

    def d_add(r2):
        dacc[...] = dacc[...] + dr[r2].astype(F32)

    others(d_pass)
    d_got(partner).wait_recv()
    d_add(partner)

    def d_add_chip(x2):
        d_add(x2 * CORES + core)
        d_got(x2 * CORES + 1 - core).wait_recv()
        d_add(x2 * CORES + 1 - core)

    others(d_add_chip)
    diag_out[0] = piv[0] - dacc[...]

    for p in range(kr):
        for j in range(cs):
            acc[p * cs + j] = pu[row * kr + p, j].astype(F32)
    for dx in range(1, n_row):
        r2 = (row + dx) % n_row
        for p in range(kr):
            pu_got(r2, p).wait_recv()
            for j in range(cs):
                acc[p * cs + j] = acc[p * cs + j] + ur[r2, p, j].astype(F32)
    for p in range(kr):
        for j in range(cs):
            upp_out[p, j] = (-acc[p * cs + j]).astype(BF)

    l_own(partner).wait_send()
    for dx in range(1, nx):
        r2 = ((x + dx) % nx) * CORES + core
        l_own(r2).wait_send()
        l_recv(r2).wait_send()
    uy_own(0).wait_send()
    uy_own(1).wait_send()

    def own_done(up):
        uz_own(up).wait_send()
        uz(z, 1, up).wait_send()

    each_dir(own_done)

    def passed(zs, up):
        uy_pass(zs).wait_send()

        @pl.when((z < nz - 1) if up else (z > 0))
        def _():
            for kind in range(2):
                uz(zs, kind, up).wait_send()

    for d in range(1, nz):
        by_side(d, passed)

    def sums_done(zd, _):
        for h in range(hp):
            ry(zd, h).wait_send()

            @pl.when(zd > z)
            def _():
                rz(zd, h, True).wait_send()

            @pl.when(zd < z)
            def _():
                rz(zd, h, False).wait_send()

        return 0

    lax.fori_loop(0, nz, sums_done, 0)

    def parts_done(k, _):
        @pl.when(k // kr != row)
        def _():
            pu_copy(k).wait_send()

        return 0

    lax.fori_loop(0, n_col, parts_done, 0)
    d_copy(partner).wait_send()

    def d_done(x2):
        d_copy(x2 * CORES + core).wait_send()
        d_relay(x2).wait_send()

    others(d_done)


def hand_over(*refs):
    for src, dst in zip(refs[:3], refs[3:]):
        dst[...] = src[...]


def body(ancestor_inv, lower_panel, upper_panel, pivot_inv, members):
    n_col = lax.axis_size("col")
    n_row = lax.axis_size("row")
    side = ancestor_inv.shape[2]
    rb, cb = ancestor_inv.shape[:2]
    kr, cs = lower_panel.shape[:2]
    per_col, rs = upper_panel.shape[:2]
    level = members.shape[0]
    nz = n_col // NY
    assert per_col == 1 and level == n_col and kr == NY and nz == n_row
    hp = 2
    nq = rs // 2
    blk = (side, side)
    dma = pltpu.SemaphoreType.DMA
    vmem = pl.BlockSpec(memory_space=pltpu.VMEM)
    hbm = pl.BlockSpec(memory_space=pltpu.HBM)
    held = rb * cb + 3 * level * cs + 2 * n_col * rs + (2 * nz + 1) * rs + n_row * (kr * cs + 1)
    limit = 2 * side * side * (held + 32)
    outs = pl.pallas_call(
        functools.partial(kernel, n_row, n_col, nq, hp),
        out_shape=(
            jax.ShapeDtypeStruct((per_col, rs) + blk, BF),
            jax.ShapeDtypeStruct((kr, cs) + blk, BF),
            jax.ShapeDtypeStruct((per_col,) + blk, F32),
        ),
        in_specs=[pl.BlockSpec(memory_space=pltpu.SMEM), hbm, hbm, hbm, vmem],
        out_specs=(vmem, vmem, vmem),
        scratch_shapes=[
            pltpu.VMEM((rb, cb) + blk, BF),
            pltpu.VMEM((level, cs) + blk, BF),
            pltpu.VMEM((n_col, rs) + blk, BF),
            pltpu.VMEM((n_col, rs) + blk, BF),
            pltpu.VMEM((nz, rs) + blk, BF),
            pltpu.VMEM((nz + 1, rs) + blk, BF),
            pltpu.VMEM((level, cs) + blk, BF),
            pltpu.VMEM((n_row, kr, cs) + blk, BF),
            pltpu.VMEM(blk, BF),
            pltpu.VMEM((n_row,) + blk, BF),
            pltpu.VMEM((max(rs, kr * cs),) + blk, F32),
            pltpu.VMEM(blk, F32),
            dma((3,)), dma((n_row,)), dma((n_row,)), dma((n_row,)),
            dma((nz + 1,)), dma((nz + 1,)), dma((nz, 2, 2)), dma((nz, 2)),
            dma((nz, hp)), dma((nz, hp)), dma((nz, hp)), dma((nz + 1, hp)),
            dma((n_col,)), dma((n_row, kr)), dma((n_row,)), dma((n_row,)),
        ],
        compiler_params=pltpu.CompilerParams(
            collective_id=0, has_side_effects=True, vmem_limit_bytes=60 * 1024 * 1024
        ),
    )(members, ancestor_inv, lower_panel, upper_panel, pivot_inv)
    return pl.pallas_call(
        hand_over,
        out_shape=tuple(jax.ShapeDtypeStruct(o.shape, o.dtype) for o in outs),
        in_specs=[vmem] * 3,
        out_specs=(vmem,) * 3,
    )(*outs)


def solution(mesh):
    return jax.shard_map(
        body,
        mesh=mesh,
        in_specs=(
            P("row", "col", None, None),
            P("row", "col", None, None),
            P("col", "row", None, None),
            P("col", None, None),
            P(),
        ),
        out_specs=(P("col", "row", None, None), P("row", "col", None, None), P("col", None, None)),
        check_vma=False,
    )
```

profile of v0, /device:TPU:11, one launch (start us, length us, event | category | flops | bytes accessed | tf_op | source)
XLA Modules:
  0.0 93.6 jit_solution(12596841127034035089)
XLA Ops:
  0.6 90.6 %shard_map.76 = (bf16[1,4,256,256]{3,2,1,0:T(8,128)(2,1)}, bf16[2,2,256,256]{3,2,1,0:T(8,128)(2,1)}, f32[1,256,256]{2,1,0:T(8,128)}) custom-call(s32[8,16]{1,0:T(8,128)} %mem.1, bf16[8,4,256,256]{3,2,1,0:T(8,128)(2,1)} %anc.1, bf16[2,2,256,256]{3,2,1,0:T(8,128)(2,1)} %low.1, bf16[1,4,256,256]{3,2,1,0:T(8,128)(2,1)} %upp.1, f32[1,256,256]{2,1,0:T(8,128)} %piv.1), custom_call_target="tpu_custom_call" | custom-call | tf_op jit(solution)/shard_map/pallas_call | solution.py:519
  91.3 2.3 %shard_map.77 = (bf16[1,4,256,256]{3,2,1,0:T(8,128)(2,1)}, bf16[2,2,256,256]{3,2,1,0:T(8,128)(2,1)}, f32[1,256,256]{2,1,0:T(8,128)}) custom-call(bf16[1,4,256,256]{3,2,1,0:T(8,128)(2,1)} %get-tuple-element.6.refs_0_, bf16[2,2,256,256]{3,2,1,0:T(8,128)(2,1)} %get-tuple-element.7.refs_1_, f32[1,256,256]{2,1,0:T(8,128)} %get-tuple-element.8.refs_2_), custom_call_target="tpu_custom_call" | custom-call | tf_op jit(solution)/shard_map/pallas_call | solution.py:550
where the time goes:
time: 93.8 us; the launch traced here: 93.6 us
  Pallas kernels  93 us (99%)
    pallas_call x1, Pallas kernels, body(): pl.pallas_call(functools.partial(kernel, n_row, n_col, nq, hp), out_shape...  90.6 us
    pallas_call x1, Pallas kernels, body(): pl.pallas_call(hand_over, out_shape=tuple((jax.ShapeDtypeStruct(o.shape,...  2.35 us

commit v1 on v0

--- a/solution.py
+++ b/solution.py
@@ -14,11 +14,12 @@
 
 
 def kernel(
-    n_row, n_col, nq, hp,
-    mem, anc, low, upp, piv,
+    n_row, n_col, nq, nf,
+    mem_in, anc, low, upp, piv_in,
     low_out, upp_out, diag_out,
-    a, lbuf, ubuf, pl_buf, yr, zr, pu, ur, ds, dr, acc, dacc,
-    loc, l_s, l_rel, l_r, uy_s, uy_r, uz_s, uz_r, ry_s, ry_r, rz_s, rz_r, pu_s, pu_r, d_s, d_r,
+    mem, piv, a, lbuf, ubuf, pl_buf, yr, zr, zq, pu, pr, ur, ds, dr, acc, dacc,
+    loc, l_s, l_rel, l_r, uy_s, uy_r, uz_s, uz_r, ry_s, ry_r, rz_s, rz_r, rq_s, rq_r,
+    pr_s, pr_r, pu_s, pu_r, d_s, d_r,
 ):
     row = lax.axis_index("row")
     col = lax.axis_index("col")
@@ -31,7 +32,7 @@
     kr, cs = low.shape[0], low.shape[1]
     rs = upp.shape[1]
     ny_blocks = rs - nq
-    hb = rs // hp
+    nyf = rs - nf
     partner = x * CORES + (1 - core)
 
     def remote(src, dst, ss, rsem, **where):
@@ -42,9 +43,13 @@
     ca = pltpu.make_async_copy(anc, a, loc.at[0])
     cl = pltpu.make_async_copy(low, lbuf.at[pl.ds(row * kr, kr)], loc.at[1])
     cu = pltpu.make_async_copy(upp.at[0], ubuf.at[col], loc.at[2])
+    cp = pltpu.make_async_copy(piv_in.at[0], piv, loc.at[3])
+    cm = pltpu.make_async_copy(mem_in, mem, loc.at[4])
+    cm.start()
     cl.start()
     cu.start()
     ca.start()
+    cp.start()
 
     bar = pltpu.get_barrier_semaphore()
     for dx in range(1, n_row):
@@ -98,26 +103,41 @@
         return remote(upp.at[0], ubuf.at[col], uz_s.at[z, int(up), 0], uz_r.at[z, 0], col=to)
 
     def ry(zd, h):
-        part = pl.ds(h * hb, hb)
         return remote(
-            pl_buf.at[zd * NY + (1 - y), part], yr.at[zd, part], ry_s.at[zd, h], ry_r.at[zd, h],
-            col=yp,
+            pl_buf.at[zd * NY + (1 - y), h], yr.at[zd, h], ry_s.at[zd, h], ry_r.at[zd, h], col=yp
         )
 
     def rz(zd, h, up):
-        part = pl.ds(h * hb, hb)
         slot = zd + 1 if up else zd
         to = col + NY if up else col - NY
         return remote(
-            pl_buf.at[zd * NY + y, part], zr.at[slot, part], rz_s.at[zd, h], rz_r.at[slot, h],
-            col=to,
+            pl_buf.at[zd * NY + y, h], zr.at[slot, h], rz_s.at[zd, h], rz_r.at[slot, h], col=to
         )
 
+    def rq(zd, f, up):
+        slot = zd + 1 if up else zd
+        to = col + NY if up else col - NY
+        return remote(
+            pl_buf.at[zd * NY + (1 - y), nyf + f], zq.at[slot, f], rq_s.at[zd, f],
+            rq_r.at[slot, f], col=to,
+        )
+
+    def pr_copy(k):
+        return remote(pu.at[k], pr.at[k], pr_s.at[k], pr_r.at[k], row=partner)
+
     def pu_copy(k):
-        return remote(pu.at[k], ur.at[row, k % kr], pu_s.at[k], pu_r.at[row, k % kr], row=k // kr)
-
-    def pu_got(r2, p):
-        return remote(pu.at[0], ur.at[r2, p], pu_s.at[0], pu_r.at[r2, p], row=r2)
+        return remote(pu.at[k], ur.at[x, k % kr], pu_s.at[k], pu_r.at[x, k % kr], row=k // kr)
+
+    def pu_got(x2, p):
+        return remote(
+            pu.at[0], ur.at[x2, p], pu_s.at[0], pu_r.at[x2, p], row=x2 * CORES + core
+        )
+
+    def keeps(k):
+        return (k // kr) % CORES == core
+
+    def leaves(k):
+        return k // (kr * CORES) != x
 
     def d_copy(r2):
         return remote(ds, dr.at[row], d_s.at[r2], d_r.at[row], row=r2)
@@ -181,8 +201,16 @@
 
         lax.fori_loop(0, cs, one, 0)
 
-        @pl.when(k // kr != row)
-        def _():
+        @pl.when(jnp.logical_not(keeps(k)))
+        def _():
+            pr_copy(k).start()
+
+    def finish(k):
+        @pl.when(jnp.logical_and(keeps(k), leaves(k)))
+        def _():
+            pr_copy(k).wait_recv()
+            for j in range(cs):
+                pu[k, j] = (pu[k, j].astype(F32) + pr[k, j].astype(F32)).astype(BF)
             pu_copy(k).start()
 
     def lower_group(r2):
@@ -192,7 +220,7 @@
 
             @pl.when(k % NY != y)
             def _():
-                for h in range(hp):
+                for h in range(nyf):
                     ry(k // NY, h).start()
 
             return 0
@@ -217,6 +245,7 @@
     uy_own(0).start()
     each_dir(lambda up: uz_own(up).start())
 
+    cm.wait()
     ca.wait()
     cl.wait()
     l_recv(partner).wait_recv()
@@ -246,15 +275,17 @@
         def _():
             fn(z + d, False)
 
-    def take(zs, up):
-        for kind in range(2):
+    def take(kind):
+        def one(zs, up):
             uz(zs, kind, up).wait_recv()
 
             @pl.when((z < nz - 1) if up else (z > 0))
             def _():
                 uz(zs, kind, up).start()
 
-    by_side(1, take)
+        return one
+
+    by_side(1, take(0))
 
     def late(x2):
         l_recv(x2 * CORES + 1 - core).wait_recv()
@@ -263,59 +294,63 @@
     others(late)
     uy_own(1).start()
     by_side(1, lambda zs, up: uy_pass(zs).start())
-
-    def near(d):
+    by_side(1, take(1))
+
+    def sides(d, fn):
         def one(s, _):
             zs = z + (2 * s - 1) * d
 
             @pl.when(jnp.logical_and(zs >= 0, zs < nz))
             def _():
-                upper_part(zs * NY + y)
+                fn(zs)
 
             return 0
 
         lax.fori_loop(0, 2, one, 0)
 
+    def near(d):
+        sides(d, lambda zs: upper_part(zs * NY + y))
+
+    def near_done(d):
+        sides(d, lambda zs: finish(zs * NY + y))
+
     def far(d):
-        def one(s, _):
-            zs = z + (2 * s - 1) * d
-
-            @pl.when(jnp.logical_and(zs >= 0, zs < nz))
+        def one(zs):
+            uy_got(1, zs).wait_recv()
+            upper_part(zs * NY + (1 - y))
+
+        sides(d, one)
+
+    def far_done(d):
+        sides(d, lambda zs: finish(zs * NY + (1 - y)))
+
+    def add_to(k, h, terms):
+        tot = pl_buf[k, h].astype(F32)
+        for t in terms:
+            tot = tot + t.astype(F32)
+        pl_buf[k, h] = tot.astype(BF)
+
+    def hop(zd, h, own, waits_y):
+        k = zd * NY + (y if own else 1 - y)
+
+        def go(up):
+            slot = zd + 1 if up else zd
+            step = rz(zd, h, up) if own else rq(zd, h - nyf, up)
+            if waits_y:
+                ry(zd, h).wait_recv()
+
+            @pl.when((z > 0) if up else (z < nz - 1))
             def _():
-                uy_got(1, zs).wait_recv()
-                upper_part(zs * NY + (1 - y))
-
-            return 0
-
-        lax.fori_loop(0, 2, one, 0)
-
-    def band_sum(zd, t):
-        k = zd * NY + y
-
-        def go(up):
-            def piece(h, _):
-                part = pl.ds(h * hb, hb)
-                ry(zd, h).wait_recv()
-
-                @pl.when((z > 0) if up else (z < nz - 1))
-                def _():
-                    rz(zd, h, up).wait_recv()
-                    slot = zd + 1 if up else zd
-                    pl_buf[k, part] = (
-                        pl_buf[k, part].astype(F32) + yr[zd, part].astype(F32)
-                        + zr[slot, part].astype(F32)
-                    ).astype(BF)
-
+                step.wait_recv()
+                part = zr[slot, h] if own else zq[slot, h - nyf]
+                add_to(k, h, [yr[zd, h], part] if waits_y else [part])
+
+            if waits_y:
                 @pl.when((z == 0) if up else (z == nz - 1))
                 def _():
-                    pl_buf[k, part] = (
-                        pl_buf[k, part].astype(F32) + yr[zd, part].astype(F32)
-                    ).astype(BF)
-
-                rz(zd, h, up).start()
-                return 0
-
-            lax.fori_loop(0, hp, piece, 0)
+                    add_to(k, h, [yr[zd, h]])
+
+            step.start()
 
         @pl.when(zd > z)
         def _():
@@ -325,24 +360,54 @@
         def _():
             go(False)
 
+    def bands(zds):
+        for f in range(nyf, rs):
+            for zd, ok in zds:
+                @pl.when(ok)
+                def _():
+                    hop(zd, f, True, False)
+                    hop(zd, f, False, False)
+
+        def piece(h, _):
+            for zd, ok in zds:
+                @pl.when(ok)
+                def _():
+                    hop(zd, h, True, True)
+
+            return 0
+
+        lax.fori_loop(0, nyf, piece, 0)
+
     def chain(t):
-        band_sum(target(t), t)
+        zd = target(t)
+        bands([(zd, zd != z)])
 
     near(1)
+    finish(col)
     edge = jnp.logical_or(z == 0, z == nz - 1)
 
     def take_pass(d):
-        by_side(d, take)
+        by_side(d, take(0))
         by_side(d, lambda zs, up: uy_pass(zs).start())
+        by_side(d, take(1))
         near(d)
-
-    def chains(t, _):
-        chain(t)
-        return 0
+        near_done(d - 1)
 
     @pl.when(edge)
     def _():
-        lax.fori_loop(0, CORES, chains, 0)
+        def first(t, _):
+            chain(t)
+            return 0
+
+        lax.fori_loop(0, CORES, first, 0)
+
+        def one(d, _):
+            chain(CORES + d - 2)
+            take_pass(d)
+            return 0
+
+        lax.fori_loop(2, nz, one, 0)
+        near_done(nz - 1)
 
     @pl.when(jnp.logical_not(edge))
     def _():
@@ -351,44 +416,58 @@
             return 0
 
         lax.fori_loop(2, nz - 1, one, 0)
-        lax.fori_loop(0, CORES, chains, 0)
-
-    @pl.when(edge)
-    def _():
-        def one(d, _):
-            take_pass(d)
-            chain(CORES + d - 2)
-            return 0
-
-        lax.fori_loop(2, nz, one, 0)
-
-    @pl.when(jnp.logical_not(edge))
-    def _():
-        lax.fori_loop(CORES, nz, chains, 0)
+        near_done(nz - 2)
+        low_half = 2 * z < nz
+        short = jnp.where(low_half, z, nz - 1 - z)
+        gap = nz - 1 - 2 * short
+
+        def pair(s, _):
+            s2 = s - gap
+            bands([
+                (jnp.where(low_half, nz - 1 - s, s), s >= 0),
+                (jnp.where(low_half, s2, nz - 1 - s2), s2 >= 0),
+            ])
+            return 0
+
+        lax.fori_loop(0, nz - 1 - short, pair, 0)
+
+    for f in range(nf):
+        k2 = z * NY + (1 - y)
+        each_dir(lambda up: rq(z, f, not up).wait_recv())
+
+        @pl.when(z > 0)
+        def _():
+            add_to(k2, nyf + f, [zq[z + 1, f]])
+
+        @pl.when(z < nz - 1)
+        def _():
+            add_to(k2, nyf + f, [zq[z, f]])
+
+        ry(z, nyf + f).start()
 
     uy_got(1, z).wait_recv()
     upper_part(yp)
     far(1)
+    finish(yp)
 
     def final(h, _):
-        part = pl.ds(h * hb, hb)
         ry(z, h).wait_recv()
-        acc[part] = pl_buf[col, part].astype(F32) + yr[z, part].astype(F32)
+        acc[h] = pl_buf[col, h].astype(F32) + yr[z, h].astype(F32)
 
         @pl.when(z > 0)
         def _():
             rz(z, h, True).wait_recv()
-            acc[part] = acc[part] + zr[z + 1, part].astype(F32)
+            acc[h] = acc[h] + zr[z + 1, h].astype(F32)
 
         @pl.when(z < nz - 1)
         def _():
             rz(z, h, False).wait_recv()
-            acc[part] = acc[part] + zr[z, part].astype(F32)
-
-        low_out[0, part] = (-acc[part]).astype(BF)
+            acc[h] = acc[h] + zr[z, h].astype(F32)
+
+        low_out[0, h] = (-acc[h]).astype(BF)
         return 0
 
-    lax.fori_loop(0, hp, final, 0)
+    lax.fori_loop(0, rs, final, 0)
     tot = None
     for i in range(rs):
         t = jnp.dot(
@@ -401,7 +480,13 @@
     others(lambda x2: d_copy(x2 * CORES + core).start())
     d_copy(partner).start()
 
-    lax.fori_loop(2, nz, lambda d, _: (far(d), 0)[1], 0)
+    def far_rest(d, _):
+        far(d)
+        far_done(d - 1)
+        return 0
+
+    lax.fori_loop(2, nz, far_rest, 0)
+    far_done(nz - 1)
 
     def d_pass(x2):
         d_got(x2 * CORES + core).wait_recv()
@@ -420,17 +505,21 @@
         d_add(x2 * CORES + 1 - core)
 
     others(d_add_chip)
-    diag_out[0] = piv[0] - dacc[...]
+    cp.wait()
+    diag_out[0] = piv[...] - dacc[...]
 
     for p in range(kr):
+        pr_copy(row * kr + p).wait_recv()
         for j in range(cs):
-            acc[p * cs + j] = pu[row * kr + p, j].astype(F32)
-    for dx in range(1, n_row):
-        r2 = (row + dx) % n_row
+            acc[p * cs + j] = pu[row * kr + p, j].astype(F32) + pr[row * kr + p, j].astype(F32)
+
+    def pu_add(x2):
         for p in range(kr):
-            pu_got(r2, p).wait_recv()
+            pu_got(x2, p).wait_recv()
             for j in range(cs):
-                acc[p * cs + j] = acc[p * cs + j] + ur[r2, p, j].astype(F32)
+                acc[p * cs + j] = acc[p * cs + j] + ur[x2, p, j].astype(F32)
+
+    others(pu_add)
     for p in range(kr):
         for j in range(cs):
             upp_out[p, j] = (-acc[p * cs + j]).astype(BF)
@@ -461,23 +550,35 @@
         by_side(d, passed)
 
     def sums_done(zd, _):
-        for h in range(hp):
+        for h in range(nyf):
             ry(zd, h).wait_send()
 
-            @pl.when(zd > z)
-            def _():
-                rz(zd, h, True).wait_send()
-
-            @pl.when(zd < z)
-            def _():
-                rz(zd, h, False).wait_send()
+        def along(up):
+            for h in range(rs):
+                rz(zd, h, up).wait_send()
+            for f in range(nf):
+                rq(zd, f, up).wait_send()
+
+        @pl.when(zd > z)
+        def _():
+            along(True)
+
+        @pl.when(zd < z)
+        def _():
+            along(False)
 
         return 0
 
     lax.fori_loop(0, nz, sums_done, 0)
+    for f in range(nf):
+        ry(z, nyf + f).wait_send()
 
     def parts_done(k, _):
-        @pl.when(k // kr != row)
+        @pl.when(jnp.logical_not(keeps(k)))
+        def _():
+            pr_copy(k).wait_send()
+
+        @pl.when(jnp.logical_and(keeps(k), leaves(k)))
         def _():
             pu_copy(k).wait_send()
 
@@ -494,8 +595,15 @@
 
 
 def hand_over(*refs):
-    for src, dst in zip(refs[:3], refs[3:]):
-        dst[...] = src[...]
+    sems = refs[-1]
+    copies = [
+        pltpu.make_async_copy(src, dst, sems.at[i])
+        for i, (src, dst) in enumerate(zip(refs[:3], refs[3:6]))
+    ]
+    for c in copies:
+        c.start()
+    for c in copies:
+        c.wait()
 
 
 def body(ancestor_inv, lower_panel, upper_panel, pivot_inv, members):
@@ -508,40 +616,43 @@
     level = members.shape[0]
     nz = n_col // NY
     assert per_col == 1 and level == n_col and kr == NY and nz == n_row
-    hp = 2
+    nf = max(1, rs // 4)
     nq = rs // 2
     blk = (side, side)
     dma = pltpu.SemaphoreType.DMA
     vmem = pl.BlockSpec(memory_space=pltpu.VMEM)
     hbm = pl.BlockSpec(memory_space=pltpu.HBM)
-    held = rb * cb + 3 * level * cs + 2 * n_col * rs + (2 * nz + 1) * rs + n_row * (kr * cs + 1)
-    limit = 2 * side * side * (held + 32)
     outs = pl.pallas_call(
-        functools.partial(kernel, n_row, n_col, nq, hp),
+        functools.partial(kernel, n_row, n_col, nq, nf),
         out_shape=(
-            jax.ShapeDtypeStruct((per_col, rs) + blk, BF),
-            jax.ShapeDtypeStruct((kr, cs) + blk, BF),
-            jax.ShapeDtypeStruct((per_col,) + blk, F32),
+            pltpu.VMEM((per_col, rs) + blk, BF),
+            pltpu.VMEM((kr, cs) + blk, BF),
+            pltpu.VMEM((per_col,) + blk, F32),
         ),
-        in_specs=[pl.BlockSpec(memory_space=pltpu.SMEM), hbm, hbm, hbm, vmem],
+        in_specs=[hbm] * 5,
         out_specs=(vmem, vmem, vmem),
         scratch_shapes=[
+            pltpu.SMEM(members.shape, jnp.int32),
+            pltpu.VMEM(blk, F32),
             pltpu.VMEM((rb, cb) + blk, BF),
             pltpu.VMEM((level, cs) + blk, BF),
             pltpu.VMEM((n_col, rs) + blk, BF),
             pltpu.VMEM((n_col, rs) + blk, BF),
             pltpu.VMEM((nz, rs) + blk, BF),
             pltpu.VMEM((nz + 1, rs) + blk, BF),
+            pltpu.VMEM((nz + 1, nf) + blk, BF),
             pltpu.VMEM((level, cs) + blk, BF),
-            pltpu.VMEM((n_row, kr, cs) + blk, BF),
+            pltpu.VMEM((level, cs) + blk, BF),
+            pltpu.VMEM((n_row // CORES, kr, cs) + blk, BF),
             pltpu.VMEM(blk, BF),
             pltpu.VMEM((n_row,) + blk, BF),
             pltpu.VMEM((max(rs, kr * cs),) + blk, F32),
             pltpu.VMEM(blk, F32),
-            dma((3,)), dma((n_row,)), dma((n_row,)), dma((n_row,)),
+            dma((5,)), dma((n_row,)), dma((n_row,)), dma((n_row,)),
             dma((nz + 1,)), dma((nz + 1,)), dma((nz, 2, 2)), dma((nz, 2)),
-            dma((nz, hp)), dma((nz, hp)), dma((nz, hp)), dma((nz + 1, hp)),
-            dma((n_col,)), dma((n_row, kr)), dma((n_row,)), dma((n_row,)),
+            dma((nz, rs)), dma((nz, rs)), dma((nz, rs)), dma((nz + 1, rs)),
+            dma((nz, nf)), dma((nz + 1, nf)), dma((n_col,)), dma((n_col,)),
+            dma((n_col,)), dma((n_row // CORES, kr)), dma((n_row,)), dma((n_row,)),
         ],
         compiler_params=pltpu.CompilerParams(
             collective_id=0, has_side_effects=True, vmem_limit_bytes=60 * 1024 * 1024
@@ -551,8 +662,9 @@
         hand_over,
         out_shape=tuple(jax.ShapeDtypeStruct(o.shape, o.dtype) for o in outs),
         in_specs=[vmem] * 3,
-        out_specs=(vmem,) * 3,
-    )(*outs)
+        out_specs=(hbm,) * 3,
+        scratch_shapes=[dma((3,))],
+    )(*(pltpu.with_memory_space_constraint(o, pltpu.VMEM) for o in outs))
 
 
 def solution(mesh):

time: 93.8 us -> 86.7 us (0.924)
  the two profiles are of different devices: /device:TPU:11 before, /device:TPU:29 now
where the time goes in v1:
time: 86.7 us; the launch traced here: 86.5 us
  Pallas kernels  85.9 us (99%)
    pallas_call x1, Pallas kernels, body(): pl.pallas_call(functools.partial(kernel, n_row, n_col, nq, nf), out_shape...  84.8 us

profile of v1, /device:TPU:29, one launch (start us, length us, event | category | flops | bytes accessed | tf_op | source)
XLA Modules:
  0.0 86.5 jit_solution(14189807802715593113)
XLA Ops:
  0.6 84.8 %shard_map.76 = (bf16[1,4,256,256]{3,2,1,0:T(8,128)(2,1)S(1)}, bf16[2,2,256,256]{3,2,1,0:T(8,128)(2,1)S(1)}, f32[1,256,256]{2,1,0:T(8,128)S(1)}) custom-call(s32[8,16]{1,0:T(8,128)} %mem_in.1, bf16[8,4,256,256]{3,2,1,0:T(8,128)(2,1)} %anc.1, bf16[2,2,256,256]{3,2,1,0:T(8,128)(2,1)} %low.1, bf16[1,4,256,256]{3,2,1,0:T(8,128)(2,1)} %upp.1, f32[1,256,256]{2,1,0:T(8,128)} %piv_in.1), custom_call_target="tpu_custom_call" | custom-call | tf_op jit(solution)/shard_map/pallas_call | solution.py:625
  85.5 1.1 %shard_map.77 = (bf16[1,4,256,256]{3,2,1,0:T(8,128)(2,1)}, bf16[2,2,256,256]{3,2,1,0:T(8,128)(2,1)}, f32[1,256,256]{2,1,0:T(8,128)}) custom-call(bf16[1,4,256,256]{3,2,1,0:T(8,128)(2,1)S(1)} %get-tuple-element.6.refs_0_, bf16[2,2,256,256]{3,2,1,0:T(8,128)(2,1)S(1)} %get-tuple-element.7.refs_1_, f32[1,256,256]{2,1,0:T(8,128)S(1)} %get-tuple-element.8.refs_2_), custom_call_target="tpu_custom_call" | custom-call | tf_op jit(solution)/shard_map/pallas_call | solution.py:661

commit v2 on v1

--- a/solution.py
+++ b/solution.py
@@ -46,8 +46,8 @@
     cp = pltpu.make_async_copy(piv_in.at[0], piv, loc.at[3])
     cm = pltpu.make_async_copy(mem_in, mem, loc.at[4])
     cm.start()
+    cu.start()
     cl.start()
-    cu.start()
     ca.start()
     cp.start()
 
@@ -68,7 +68,8 @@
     pl.semaphore_wait(bar, peers)
 
     def l_own(r2):
-        return remote(low, lbuf.at[pl.ds(row * kr, kr)], l_s.at[r2], l_r.at[row], row=r2)
+        blk = lbuf.at[pl.ds(row * kr, kr)]
+        return remote(blk, blk, l_s.at[r2], l_r.at[row], row=r2)
 
     def l_recv(r2):
         blk = lbuf.at[pl.ds(r2 * kr, kr)]
@@ -77,7 +78,7 @@
     def uy_own(kind):
         part = pl.ds(0, ny_blocks) if kind else pl.ds(ny_blocks, nq)
         return remote(
-            upp.at[0, part], ubuf.at[col, part], uy_s.at[nz if kind == 0 else z],
+            ubuf.at[col, part], ubuf.at[col, part], uy_s.at[nz if kind == 0 else z],
             uy_r.at[nz if kind == 0 else z], col=yp,
         )
 
@@ -100,7 +101,7 @@
 
     def uz_own(up):
         to = col + NY if up else col - NY
-        return remote(upp.at[0], ubuf.at[col], uz_s.at[z, int(up), 0], uz_r.at[z, 0], col=to)
+        return remote(ubuf.at[col], ubuf.at[col], uz_s.at[z, int(up), 0], uz_r.at[z, 0], col=to)
 
     def ry(zd, h):
         return remote(
@@ -166,6 +167,29 @@
     def col_member(k, j):
         m = mem[k, col * cs + j]
         return m >= 0, jnp.clip(m - col * cb, 0, cb - 1)
+
+    planes = nz // nx
+    edge = jnp.logical_or(z == 0, z == nz - 1)
+
+    def mine(zs):
+        return zs // planes == x
+
+    def last_to(up):
+        e = nz - 1 if up else 0
+        return jnp.where(mine(e), nz - 2 if up else 1, nz - 1 - e)
+
+    def held_back(zs, up):
+        return jnp.logical_and(z == (nz - 2 if up else 1), zs == last_to(up))
+
+    def order(i):
+        near_half = jnp.where(i % 2 == 0, nz // 2 + i // 2, i // 2)
+        dist = jnp.where(mine(z), near_half, i)
+        inner_low = jnp.where(i < nz // 2, nz // 2 + i, nz - 1 - i)
+        inner_high = jnp.where(i < nz // 2, nz // 2 - 1 - i, i)
+        return jnp.where(
+            edge, jnp.where(z == 0, dist, nz - 1 - dist),
+            jnp.where(2 * x < nx, inner_low, inner_high),
+        )
 
     zero = jnp.zeros((), BF)
 
@@ -227,11 +251,6 @@
 
         lax.fori_loop(0, kr, one, 0)
 
-    def target(t):
-        x2 = (x + t // CORES) % nx
-        q = t % CORES
-        return x2 * CORES + jnp.where(2 * x2 >= nx, CORES - 1 - q, q)
-
     def both_groups(x2):
         def one(q, _):
             lower_group(x2 * CORES + jnp.where(2 * x2 >= nx, CORES - 1 - q, q))
@@ -239,21 +258,26 @@
 
         lax.fori_loop(0, CORES, one, 0)
 
+    cu.wait()
+    uy_own(0).start()
+    each_dir(lambda up: uz_own(up).start())
+    cl.wait()
     l_own(partner).start()
     for dx in range(1, nx):
         l_own(((x + dx) % nx) * CORES + core).start()
-    uy_own(0).start()
-    each_dir(lambda up: uz_own(up).start())
-
     cm.wait()
     ca.wait()
-    cl.wait()
     l_recv(partner).wait_recv()
     both_groups(x)
 
     uy_got(0, z).wait_recv()
-    each_dir(lambda up: uz(z, 1, up).start())
-    cu.wait()
+
+    def share(zs, up):
+        @pl.when(jnp.logical_not(held_back(zs, up)))
+        def _():
+            uz(zs, 1, up).start()
+
+    each_dir(lambda up: share(z, up))
     upper_part(col)
 
     def others(fn):
@@ -281,7 +305,10 @@
 
             @pl.when((z < nz - 1) if up else (z > 0))
             def _():
-                uz(zs, kind, up).start()
+                if kind:
+                    share(zs, up)
+                else:
+                    uz(zs, kind, up).start()
 
         return one
 
@@ -292,9 +319,19 @@
         both_groups(x2)
 
     others(late)
-    uy_own(1).start()
-    by_side(1, lambda zs, up: uy_pass(zs).start())
-    by_side(1, take(1))
+
+    @pl.when(jnp.logical_not(edge))
+    def _():
+        by_side(1, take(1))
+
+    def hand_on(zs):
+        @pl.when(zs == z)
+        def _():
+            uy_own(1).start()
+
+        @pl.when(zs != z)
+        def _():
+            uy_pass(zs).start()
 
     def sides(d, fn):
         def one(s, _):
@@ -314,15 +351,37 @@
     def near_done(d):
         sides(d, lambda zs: finish(zs * NY + y))
 
-    def far(d):
-        def one(zs):
-            uy_got(1, zs).wait_recv()
-            upper_part(zs * NY + (1 - y))
-
-        sides(d, one)
-
-    def far_done(d):
-        sides(d, lambda zs: finish(zs * NY + (1 - y)))
+    def across(i):
+        zs = order(i)
+
+        @pl.when(jnp.logical_and(edge, zs > z))
+        def _():
+            uz(zs, 1, False).wait_recv()
+
+        @pl.when(jnp.logical_and(edge, zs < z))
+        def _():
+            uz(zs, 1, True).wait_recv()
+
+        uy_got(1, zs).wait_recv()
+        upper_part(zs * NY + (1 - y))
+
+    def across_done(i):
+        finish(order(i) * NY + (1 - y))
+
+    def home():
+        k2 = z * NY + (1 - y)
+        for f in range(nf):
+            each_dir(lambda up: rq(z, f, not up).wait_recv())
+
+            @pl.when(z > 0)
+            def _():
+                add_to(k2, nyf + f, [zq[z + 1, f]])
+
+            @pl.when(z < nz - 1)
+            def _():
+                add_to(k2, nyf + f, [zq[z, f]])
+
+            ry(z, nyf + f).start()
 
     def add_to(k, h, terms):
         tot = pl_buf[k, h].astype(F32)
@@ -360,7 +419,7 @@
         def _():
             go(False)
 
-    def bands(zds):
+    def firsts(zds):
         for f in range(nyf, rs):
             for zd, ok in zds:
                 @pl.when(ok)
@@ -368,87 +427,149 @@
                     hop(zd, f, True, False)
                     hop(zd, f, False, False)
 
+    def seconds(zds, hook=None, close=None):
         def piece(h, _):
+            if hook is not None:
+                hook(h)
             for zd, ok in zds:
                 @pl.when(ok)
                 def _():
                     hop(zd, h, True, True)
 
+                if close is not None and zd is zds[0][0]:
+                    @pl.when(h == nyf - 1)
+                    def _():
+                        close()
+
             return 0
 
         lax.fori_loop(0, nyf, piece, 0)
-
-    def chain(t):
-        zd = target(t)
-        bands([(zd, zd != z)])
 
     near(1)
     finish(col)
-    edge = jnp.logical_or(z == 0, z == nz - 1)
-
-    def take_pass(d):
-        by_side(d, take(0))
-        by_side(d, lambda zs, up: uy_pass(zs).start())
-        by_side(d, take(1))
-        near(d)
-        near_done(d - 1)
 
     @pl.when(edge)
     def _():
-        def first(t, _):
-            chain(t)
-            return 0
-
-        lax.fori_loop(0, CORES, first, 0)
+        def ends(j):
+            return [(jnp.where(z == 0, nz - 1 - j, j), j < nz - 1)]
+
+        def opening(j, _):
+            firsts(ends(j))
+            return 0
+
+        lax.fori_loop(0, 2, opening, 0)
+        seconds(ends(0))
+
+        def on(dist):
+            hand_on(jnp.where(z == 0, dist, nz - 1 - dist))
 
         def one(d, _):
-            chain(CORES + d - 2)
-            take_pass(d)
+            by_side(d, take(0))
+
+            @pl.when(jnp.logical_and(mine(z), d >= nz // 2))
+            def _():
+                on(d)
+
+                @pl.when(d < nz - 1)
+                def _():
+                    on(d - nz // 2)
+
+            @pl.when(jnp.logical_not(mine(z)))
+            def _():
+                @pl.when(d == 2)
+                def _():
+                    on(0)
+                    on(1)
+
+                @pl.when(d < nz - 1)
+                def _():
+                    on(d)
+
+            near(d)
+            near_done(d - 1)
+            seconds(ends(d - 1))
+            firsts(ends(d))
             return 0
 
         lax.fori_loop(2, nz, one, 0)
+        across(0)
         near_done(nz - 1)
+        home()
+        hand_on(order(nz - 1))
+        across(1)
+        across_done(0)
 
     @pl.when(jnp.logical_not(edge))
     def _():
         def one(d, _):
-            take_pass(d)
+            by_side(d, take(0))
+            by_side(d, take(1))
+            near(d)
+            near_done(d - 1)
             return 0
 
         lax.fori_loop(2, nz - 1, one, 0)
+        for i in range(nz - 1):
+            hand_on(order(i))
         near_done(nz - 2)
         low_half = 2 * z < nz
         short = jnp.where(low_half, z, nz - 1 - z)
         gap = nz - 1 - 2 * short
+        spot = nyf - 2
 
         def pair(s, _):
             s2 = s - gap
-            bands([
+
+            def hook(h):
+                now = s == nz - 2 - short
+
+                @pl.when(jnp.logical_and(now, h - spot == 0))
+                def _():
+                    across(0)
+
+                @pl.when(jnp.logical_and(now, h - spot == 1))
+                def _():
+                    across(1)
+
+            def close():
+                @pl.when(s2 == short - 1)
+                def _():
+                    @pl.when(z == 1)
+                    def _():
+                        uz(last_to(False), 1, False).start()
+
+                    @pl.when(z == nz - 2)
+                    def _():
+                        uz(last_to(True), 1, True).start()
+
+            both = [
+                (
+                    jnp.where(low_half, s2, nz - 1 - s2),
+                    jnp.logical_and(s2 >= 0, s2 < short),
+                ),
                 (jnp.where(low_half, nz - 1 - s, s), s >= 0),
-                (jnp.where(low_half, s2, nz - 1 - s2), s2 >= 0),
-            ])
+            ]
+            firsts(both)
+            seconds(both, hook, close)
             return 0
 
         lax.fori_loop(0, nz - 1 - short, pair, 0)
-
-    for f in range(nf):
-        k2 = z * NY + (1 - y)
-        each_dir(lambda up: rq(z, f, not up).wait_recv())
-
-        @pl.when(z > 0)
-        def _():
-            add_to(k2, nyf + f, [zq[z + 1, f]])
-
-        @pl.when(z < nz - 1)
-        def _():
-            add_to(k2, nyf + f, [zq[z, f]])
-
-        ry(z, nyf + f).start()
-
-    uy_got(1, z).wait_recv()
-    upper_part(yp)
-    far(1)
-    finish(yp)
+        home()
+        hand_on(order(nz - 1))
+        across_done(0)
+
+    across_done(1)
+
+    def rest(i, _):
+        across(i)
+
+        @pl.when(i > 2)
+        def _():
+            across_done(i - 1)
+
+        return 0
+
+    lax.fori_loop(2, nz - 1, rest, 0)
 
     def final(h, _):
         ry(z, h).wait_recv()
@@ -480,13 +601,10 @@
     others(lambda x2: d_copy(x2 * CORES + core).start())
     d_copy(partner).start()
 
-    def far_rest(d, _):
-        far(d)
-        far_done(d - 1)
-        return 0
-
-    lax.fori_loop(2, nz, far_rest, 0)
-    far_done(nz - 1)
+    across_done(nz - 2)
+    across(nz - 1)
+    across_done(nz - 1)
+
 
     def d_pass(x2):
         d_got(x2 * CORES + core).wait_recv()
@@ -615,7 +733,7 @@
     per_col, rs = upper_panel.shape[:2]
     level = members.shape[0]
     nz = n_col // NY
-    assert per_col == 1 and level == n_col and kr == NY and nz == n_row
+    assert per_col == 1 and level == n_col and kr == NY and nz == n_row and rs >= 4
     nf = max(1, rs // 4)
     nq = rs // 2
     blk = (side, side)

time: 86.7 us -> 78.9 us (0.910)
  the two profiles are of different devices: /device:TPU:29 before, /device:TPU:19 now
where the time goes in v2:
time: 78.9 us; the launch traced here: 78.7 us
  Pallas kernels  78.1 us (99%)
    pallas_call x1, Pallas kernels, body(): pl.pallas_call(functools.partial(kernel, n_row, n_col, nq, nf), out_shape...  77 us

profile of v2, /device:TPU:19, one launch (start us, length us, event | category | flops | bytes accessed | tf_op | source)
XLA Modules:
  0.0 78.7 jit_solution(8453349651790742945)
XLA Ops:
  0.6 77.0 %shard_map.76 = (bf16[1,4,256,256]{3,2,1,0:T(8,128)(2,1)S(1)}, bf16[2,2,256,256]{3,2,1,0:T(8,128)(2,1)S(1)}, f32[1,256,256]{2,1,0:T(8,128)S(1)}) custom-call(s32[8,16]{1,0:T(8,128)} %mem_in.1, bf16[8,4,256,256]{3,2,1,0:T(8,128)(2,1)} %anc.1, bf16[2,2,256,256]{3,2,1,0:T(8,128)(2,1)} %low.1, bf16[1,4,256,256]{3,2,1,0:T(8,128)(2,1)} %upp.1, f32[1,256,256]{2,1,0:T(8,128)} %piv_in.1), custom_call_target="tpu_custom_call" | custom-call | tf_op jit(solution)/shard_map/pallas_call | solution.py:743
  77.7 1.1 %shard_map.77 = (bf16[1,4,256,256]{3,2,1,0:T(8,128)(2,1)}, bf16[2,2,256,256]{3,2,1,0:T(8,128)(2,1)}, f32[1,256,256]{2,1,0:T(8,128)}) custom-call(bf16[1,4,256,256]{3,2,1,0:T(8,128)(2,1)S(1)} %get-tuple-element.6.refs_0_, bf16[2,2,256,256]{3,2,1,0:T(8,128)(2,1)S(1)} %get-tuple-element.7.refs_1_, f32[1,256,256]{2,1,0:T(8,128)S(1)} %get-tuple-element.8.refs_2_), custom_call_target="tpu_custom_call" | custom-call | tf_op jit(solution)/shard_map/pallas_call | solution.py:779

commit v3 on v2

--- a/solution.py
+++ b/solution.py
@@ -18,8 +18,7 @@
     mem_in, anc, low, upp, piv_in,
     low_out, upp_out, diag_out,
     mem, piv, a, lbuf, ubuf, pl_buf, yr, zr, zq, pu, pr, ur, ds, dr, acc, dacc,
-    loc, l_s, l_rel, l_r, uy_s, uy_r, uz_s, uz_r, ry_s, ry_r, rz_s, rz_r, rq_s, rq_r,
-    pr_s, pr_r, pu_s, pu_r, d_s, d_r,
+    loc, sent, l_r, uy_r, uz_r, ry_r, rz_r, rq_r, pr_r, pu_r, d_r,
 ):
     row = lax.axis_index("row")
     col = lax.axis_index("col")
@@ -67,71 +66,68 @@
     peers = n_row + jnp.where(z > 0, 1, 0) + jnp.where(z < nz - 1, 1, 0)
     pl.semaphore_wait(bar, peers)
 
+    L_S, UY_S, RY_S, RH_S, RZ_S, RQ_S, PR_S, PU_S, D_S, UZ_S = range(10)
+
     def l_own(r2):
         blk = lbuf.at[pl.ds(row * kr, kr)]
-        return remote(blk, blk, l_s.at[r2], l_r.at[row], row=r2)
+        return remote(blk, blk, sent.at[L_S], l_r.at[row], row=r2)
 
     def l_recv(r2):
         blk = lbuf.at[pl.ds(r2 * kr, kr)]
-        return remote(blk, blk, l_rel.at[r2], l_r.at[r2], row=partner)
+        return remote(blk, blk, sent.at[L_S], l_r.at[r2], row=partner)
+
+    def uy(k, late, rsem):
+        part = pl.ds(0, ny_blocks) if late else pl.ds(ny_blocks, nq)
+        blk = ubuf.at[k, part]
+        return remote(blk, blk, sent.at[UY_S], uy_r.at[rsem], col=yp)
 
     def uy_own(kind):
-        part = pl.ds(0, ny_blocks) if kind else pl.ds(ny_blocks, nq)
+        return uy(col, kind == 1, z if kind else nz)
+
+    def uy_got(kind, zs):
+        return uy(zs * NY + (1 - y), kind == 1, zs if kind else nz)
+
+    def uy_pass(zs):
+        return uy(zs * NY + y, True, zs)
+
+    def uz(zs, kind, up):
+        k = zs * NY + (1 - y if kind == 2 else y)
+        blk = ubuf.at[k, pl.ds(0, ny_blocks) if kind == 0 else pl.ds(ny_blocks, nq)]
+        to = col + NY if up else col - NY
+        return remote(blk, blk, sent.at[UZ_S + kind], uz_r.at[zs, kind], col=to)
+
+    def ry_at(zd, h, ssem):
         return remote(
-            ubuf.at[col, part], ubuf.at[col, part], uy_s.at[nz if kind == 0 else z],
-            uy_r.at[nz if kind == 0 else z], col=yp,
+            pl_buf.at[zd * NY + (1 - y), h], yr.at[zd, h], sent.at[ssem], ry_r.at[zd, h], col=yp
         )
 
-    def uy_got(kind, zs):
-        part = pl.ds(0, ny_blocks) if kind else pl.ds(ny_blocks, nq)
-        blk = ubuf.at[zs * NY + (1 - y), part]
-        return remote(blk, blk, uy_s.at[zs], uy_r.at[nz if kind == 0 else zs], col=yp)
-
-    def uy_pass(zs):
-        blk = ubuf.at[zs * NY + y, pl.ds(0, ny_blocks)]
-        return remote(blk, blk, uy_s.at[zs], uy_r.at[zs], col=yp)
-
-    def uz(zs, kind, up):
-        if kind == 0:
-            blk = ubuf.at[zs * NY + y]
-        else:
-            blk = ubuf.at[zs * NY + (1 - y), pl.ds(ny_blocks, nq)]
-        to = col + NY if up else col - NY
-        return remote(blk, blk, uz_s.at[zs, int(up), kind], uz_r.at[zs, kind], col=to)
-
-    def uz_own(up):
-        to = col + NY if up else col - NY
-        return remote(ubuf.at[col], ubuf.at[col], uz_s.at[z, int(up), 0], uz_r.at[z, 0], col=to)
-
     def ry(zd, h):
-        return remote(
-            pl_buf.at[zd * NY + (1 - y), h], yr.at[zd, h], ry_s.at[zd, h], ry_r.at[zd, h], col=yp
-        )
+        return ry_at(zd, h, RY_S)
 
     def rz(zd, h, up):
         slot = zd + 1 if up else zd
         to = col + NY if up else col - NY
         return remote(
-            pl_buf.at[zd * NY + y, h], zr.at[slot, h], rz_s.at[zd, h], rz_r.at[slot, h], col=to
+            pl_buf.at[zd * NY + y, h], zr.at[slot, h], sent.at[RZ_S], rz_r.at[slot, h], col=to
         )
 
     def rq(zd, f, up):
         slot = zd + 1 if up else zd
         to = col + NY if up else col - NY
         return remote(
-            pl_buf.at[zd * NY + (1 - y), nyf + f], zq.at[slot, f], rq_s.at[zd, f],
+            pl_buf.at[zd * NY + (1 - y), nyf + f], zq.at[slot, f], sent.at[RQ_S],
             rq_r.at[slot, f], col=to,
         )
 
     def pr_copy(k):
-        return remote(pu.at[k], pr.at[k], pr_s.at[k], pr_r.at[k], row=partner)
+        return remote(pu.at[k], pr.at[k], sent.at[PR_S], pr_r.at[k], row=partner)
 
     def pu_copy(k):
-        return remote(pu.at[k], ur.at[x, k % kr], pu_s.at[k], pu_r.at[x, k % kr], row=k // kr)
+        return remote(pu.at[k], ur.at[x, k % kr], sent.at[PU_S], pu_r.at[x, k % kr], row=k // kr)
 
     def pu_got(x2, p):
         return remote(
-            pu.at[0], ur.at[x2, p], pu_s.at[0], pu_r.at[x2, p], row=x2 * CORES + core
+            pu.at[0], ur.at[x2, p], sent.at[PU_S], pu_r.at[x2, p], row=x2 * CORES + core
         )
 
     def keeps(k):
@@ -141,15 +137,15 @@
         return k // (kr * CORES) != x
 
     def d_copy(r2):
-        return remote(ds, dr.at[row], d_s.at[r2], d_r.at[row], row=r2)
+        return remote(ds, dr.at[row], sent.at[D_S], d_r.at[row], row=r2)
 
     def d_got(r2):
-        return remote(ds, dr.at[r2], d_s.at[r2], d_r.at[r2], row=r2)
+        return remote(ds, dr.at[r2], sent.at[D_S], d_r.at[r2], row=r2)
 
     def d_relay(x2):
         r2 = x2 * CORES + core
         blk = dr.at[r2]
-        return remote(blk, blk, d_s.at[x2 * CORES + 1 - core], d_r.at[r2], row=partner)
+        return remote(blk, blk, sent.at[D_S], d_r.at[r2], row=partner)
 
     def each_dir(fn):
         @pl.when(z > 0)
@@ -260,7 +256,8 @@
 
     cu.wait()
     uy_own(0).start()
-    each_dir(lambda up: uz_own(up).start())
+    each_dir(lambda up: uz(z, 0, up).start())
+    each_dir(lambda up: uz(z, 1, up).start())
     cl.wait()
     l_own(partner).start()
     for dx in range(1, nx):
@@ -275,7 +272,7 @@
     def share(zs, up):
         @pl.when(jnp.logical_not(held_back(zs, up)))
         def _():
-            uz(zs, 1, up).start()
+            uz(zs, 2, up).start()
 
     each_dir(lambda up: share(z, up))
     upper_part(col)
@@ -288,8 +285,6 @@
         l_recv(x2 * CORES + core).wait_recv()
         l_recv(x2 * CORES + core).start()
 
-    others(relay)
-
     def by_side(d, fn):
         @pl.when(z - d >= 0)
         def _():
@@ -305,7 +300,7 @@
 
             @pl.when((z < nz - 1) if up else (z > 0))
             def _():
-                if kind:
+                if kind == 2:
                     share(zs, up)
                 else:
                     uz(zs, kind, up).start()
@@ -313,6 +308,8 @@
         return one
 
     by_side(1, take(0))
+    others(relay)
+    by_side(1, take(1))
 
     def late(x2):
         l_recv(x2 * CORES + 1 - core).wait_recv()
@@ -322,7 +319,7 @@
 
     @pl.when(jnp.logical_not(edge))
     def _():
-        by_side(1, take(1))
+        by_side(1, take(2))
 
     def hand_on(zs):
         @pl.when(zs == z)
@@ -356,11 +353,11 @@
 
         @pl.when(jnp.logical_and(edge, zs > z))
         def _():
-            uz(zs, 1, False).wait_recv()
+            uz(zs, 2, False).wait_recv()
 
         @pl.when(jnp.logical_and(edge, zs < z))
         def _():
-            uz(zs, 1, True).wait_recv()
+            uz(zs, 2, True).wait_recv()
 
         uy_got(1, zs).wait_recv()
         upper_part(zs * NY + (1 - y))
@@ -381,7 +378,7 @@
             def _():
                 add_to(k2, nyf + f, [zq[z, f]])
 
-            ry(z, nyf + f).start()
+            ry_at(z, nyf + f, RH_S).start()
 
     def add_to(k, h, terms):
         tot = pl_buf[k, h].astype(F32)
@@ -485,6 +482,7 @@
                 def _():
                     on(d)
 
+            by_side(d, take(1))
             near(d)
             near_done(d - 1)
             seconds(ends(d - 1))
@@ -501,9 +499,18 @@
 
     @pl.when(jnp.logical_not(edge))
     def _():
+        low_half = 2 * z < nz
+        short = jnp.where(low_half, z, nz - 1 - z)
+
         def one(d, _):
             by_side(d, take(0))
             by_side(d, take(1))
+
+            @pl.when(d == nz - 2)
+            def _():
+                firsts([(jnp.where(low_half, nz - 1, 0), d > 0)])
+
+            by_side(d, take(2))
             near(d)
             near_done(d - 1)
             return 0
@@ -511,9 +518,6 @@
         lax.fori_loop(2, nz - 1, one, 0)
         for i in range(nz - 1):
             hand_on(order(i))
-        near_done(nz - 2)
-        low_half = 2 * z < nz
-        short = jnp.where(low_half, z, nz - 1 - z)
         gap = nz - 1 - 2 * short
         spot = nyf - 2
 
@@ -525,6 +529,7 @@
 
                 @pl.when(jnp.logical_and(now, h - spot == 0))
                 def _():
+                    near_done(nz - 2)
                     across(0)
 
                 @pl.when(jnp.logical_and(now, h - spot == 1))
@@ -536,11 +541,11 @@
                 def _():
                     @pl.when(z == 1)
                     def _():
-                        uz(last_to(False), 1, False).start()
+                        uz(last_to(False), 2, False).start()
 
                     @pl.when(z == nz - 2)
                     def _():
-                        uz(last_to(True), 1, True).start()
+                        uz(last_to(True), 2, True).start()
 
             both = [
                 (
@@ -549,7 +554,7 @@
                 ),
                 (jnp.where(low_half, nz - 1 - s, s), s >= 0),
             ]
-            firsts(both)
+            firsts([both[0], (both[1][0], s > 0)])
             seconds(both, hook, close)
             return 0
 
@@ -602,30 +607,17 @@
     d_copy(partner).start()
 
     across_done(nz - 2)
-    across(nz - 1)
-    across_done(nz - 1)
-
 
     def d_pass(x2):
         d_got(x2 * CORES + core).wait_recv()
         d_relay(x2).start()
 
-    def d_add(r2):
-        dacc[...] = dacc[...] + dr[r2].astype(F32)
-
-    others(d_pass)
-    d_got(partner).wait_recv()
-    d_add(partner)
-
-    def d_add_chip(x2):
-        d_add(x2 * CORES + core)
-        d_got(x2 * CORES + 1 - core).wait_recv()
-        d_add(x2 * CORES + 1 - core)
-
-    others(d_add_chip)
-    cp.wait()
-    diag_out[0] = piv[...] - dacc[...]
-
+    @pl.when(edge)
+    def _():
+        others(d_pass)
+
+    across(nz - 1)
+    across_done(nz - 1)
     for p in range(kr):
         pr_copy(row * kr + p).wait_recv()
         for j in range(cs):
@@ -642,74 +634,46 @@
         for j in range(cs):
             upp_out[p, j] = (-acc[p * cs + j]).astype(BF)
 
-    l_own(partner).wait_send()
-    for dx in range(1, nx):
-        r2 = ((x + dx) % nx) * CORES + core
-        l_own(r2).wait_send()
-        l_recv(r2).wait_send()
-    uy_own(0).wait_send()
-    uy_own(1).wait_send()
-
-    def own_done(up):
-        uz_own(up).wait_send()
-        uz(z, 1, up).wait_send()
-
-    each_dir(own_done)
-
-    def passed(zs, up):
-        uy_pass(zs).wait_send()
-
-        @pl.when((z < nz - 1) if up else (z > 0))
-        def _():
-            for kind in range(2):
-                uz(zs, kind, up).wait_send()
-
-    for d in range(1, nz):
-        by_side(d, passed)
-
-    def sums_done(zd, _):
-        for h in range(nyf):
-            ry(zd, h).wait_send()
-
-        def along(up):
-            for h in range(rs):
-                rz(zd, h, up).wait_send()
-            for f in range(nf):
-                rq(zd, f, up).wait_send()
-
-        @pl.when(zd > z)
-        def _():
-            along(True)
-
-        @pl.when(zd < z)
-        def _():
-            along(False)
-
-        return 0
-
-    lax.fori_loop(0, nz, sums_done, 0)
-    for f in range(nf):
-        ry(z, nyf + f).wait_send()
-
-    def parts_done(k, _):
-        @pl.when(jnp.logical_not(keeps(k)))
-        def _():
-            pr_copy(k).wait_send()
-
-        @pl.when(jnp.logical_and(keeps(k), leaves(k)))
-        def _():
-            pu_copy(k).wait_send()
-
-        return 0
-
-    lax.fori_loop(0, n_col, parts_done, 0)
-    d_copy(partner).wait_send()
-
-    def d_done(x2):
-        d_copy(x2 * CORES + core).wait_send()
-        d_relay(x2).wait_send()
-
-    others(d_done)
+    def all_sent(ref, which):
+        pltpu.make_async_copy(ref, ref, sent.at[which]).wait()
+
+    for kind in range(3):
+        @pl.when(edge)
+        def _():
+            all_sent(ubuf.at[pl.ds(0, 1), pl.ds(0, nq)], UZ_S + kind)
+
+        @pl.when(jnp.logical_not(edge))
+        def _():
+            all_sent(ubuf.at[pl.ds(0, nz + 1), pl.ds(0, nq)], UZ_S + kind)
+
+    all_sent(lbuf.at[pl.ds(0, kr * (2 * nx - 1))], L_S)
+    all_sent(ubuf.at[pl.ds(0, nz + 1), pl.ds(0, nq)], UY_S)
+    all_sent(pl_buf.at[pl.ds(0, nz), pl.ds(0, nyf)], RY_S)
+    all_sent(pl_buf.at[pl.ds(0, 1), pl.ds(0, nf)], RH_S)
+    all_sent(pl_buf.at[pl.ds(0, nz - 1)], RZ_S)
+    all_sent(pl_buf.at[pl.ds(0, nz - 1), pl.ds(0, nf)], RQ_S)
+    all_sent(pu.at[pl.ds(0, n_col // CORES)], PR_S)
+    all_sent(pu.at[pl.ds(0, kr * (nx - 1))], PU_S)
+
+    @pl.when(jnp.logical_not(edge))
+    def _():
+        others(d_pass)
+
+    def d_add(r2):
+        dacc[...] = dacc[...] + dr[r2].astype(F32)
+
+    d_got(partner).wait_recv()
+    d_add(partner)
+
+    def d_add_chip(x2):
+        d_add(x2 * CORES + core)
+        d_got(x2 * CORES + 1 - core).wait_recv()
+        d_add(x2 * CORES + 1 - core)
+
+    others(d_add_chip)
+    cp.wait()
+    diag_out[0] = piv[...] - dacc[...]
+    all_sent(dr.at[pl.ds(0, 2 * nx - 1)], D_S)
 
 
 def hand_over(*refs):
@@ -733,7 +697,7 @@
     per_col, rs = upper_panel.shape[:2]
     level = members.shape[0]
     nz = n_col // NY
-    assert per_col == 1 and level == n_col and kr == NY and nz == n_row and rs >= 4
+    assert per_col == 1 and level == n_col and kr == NY and nz == n_row and rs >= 4 and rs % 2 == 0
     nf = max(1, rs // 4)
     nq = rs // 2
     blk = (side, side)
@@ -766,11 +730,9 @@
             pltpu.VMEM((n_row,) + blk, BF),
             pltpu.VMEM((max(rs, kr * cs),) + blk, F32),
             pltpu.VMEM(blk, F32),
-            dma((5,)), dma((n_row,)), dma((n_row,)), dma((n_row,)),
-            dma((nz + 1,)), dma((nz + 1,)), dma((nz, 2, 2)), dma((nz, 2)),
-            dma((nz, rs)), dma((nz, rs)), dma((nz, rs)), dma((nz + 1, rs)),
-            dma((nz, nf)), dma((nz + 1, nf)), dma((n_col,)), dma((n_col,)),
-            dma((n_col,)), dma((n_row // CORES, kr)), dma((n_row,)), dma((n_row,)),
+            dma((5,)), dma((12,)), dma((n_row,)), dma((nz + 1,)), dma((nz, 3)),
+            dma((nz, rs)), dma((nz + 1, rs)), dma((nz + 1, nf)), dma((n_col,)),
+            dma((n_row // CORES, kr)), dma((n_row,)),
         ],
         compiler_params=pltpu.CompilerParams(
             collective_id=0, has_side_effects=True, vmem_limit_bytes=60 * 1024 * 1024

time: 78.9 us -> 75.3 us (0.954)
  the two profiles are of different devices: /device:TPU:19 before, /device:TPU:11 now
where the time goes in v3:
time: 75.3 us; the launch traced here: 74.3 us
  Pallas kernels  73.7 us (98%)
    pallas_call x1, Pallas kernels, body(): pl.pallas_call(functools.partial(kernel, n_row, n_col, nq, nf), out_shape...  72.6 us

profile of v3, /device:TPU:11, one launch (start us, length us, event | category | flops | bytes accessed | tf_op | source)
XLA Modules:
  0.0 74.3 jit_solution(6212445925168042480)
XLA Ops:
  0.6 72.6 %shard_map.76 = (bf16[1,4,256,256]{3,2,1,0:T(8,128)(2,1)S(1)}, bf16[2,2,256,256]{3,2,1,0:T(8,128)(2,1)S(1)}, f32[1,256,256]{2,1,0:T(8,128)S(1)}) custom-call(s32[8,16]{1,0:T(8,128)} %mem_in.1, bf16[8,4,256,256]{3,2,1,0:T(8,128)(2,1)} %anc.1, bf16[2,2,256,256]{3,2,1,0:T(8,128)(2,1)} %low.1, bf16[1,4,256,256]{3,2,1,0:T(8,128)(2,1)} %upp.1, f32[1,256,256]{2,1,0:T(8,128)} %piv_in.1), custom_call_target="tpu_custom_call" | custom-call | tf_op jit(solution)/shard_map/pallas_call | solution.py:707
  73.3 1.1 %shard_map.77 = (bf16[1,4,256,256]{3,2,1,0:T(8,128)(2,1)}, bf16[2,2,256,256]{3,2,1,0:T(8,128)(2,1)}, f32[1,256,256]{2,1,0:T(8,128)}) custom-call(bf16[1,4,256,256]{3,2,1,0:T(8,128)(2,1)S(1)} %get-tuple-element.6.refs_0_, bf16[2,2,256,256]{3,2,1,0:T(8,128)(2,1)S(1)} %get-tuple-element.7.refs_1_, f32[1,256,256]{2,1,0:T(8,128)S(1)} %get-tuple-element.8.refs_2_), custom_call_target="tpu_custom_call" | custom-call | tf_op jit(solution)/shard_map/pallas_call | solution.py:741

commit v4 on v3

v4 whole, which is shorter than its diff:
```python
import functools

import jax
import jax.numpy as jnp
from jax import lax
from jax.experimental import pallas as pl
from jax.experimental.pallas import tpu as pltpu
from jax.sharding import PartitionSpec as P

NY = 2
CORES = 2
BF = jnp.bfloat16
F32 = jnp.float32


def kernel(
    n_row, n_col, nq, nf, pz, nyp, py,
    mem_in, anc, low, upp, piv_in,
    low_out, upp_out, diag_out,
    mem, piv, a, lbuf, ubuf, pl_buf, yr, zr, zq, pu, pr, ur, ds, dr, acc, dacc,
    loc, sent, l_r, uy_r, uz_r, ry_r, rh_r, rz_r, rf_r, rq_r,
    pr_r, pu_r, d_r,
):
    row = lax.axis_index("row")
    col = lax.axis_index("col")
    nz = n_col // NY
    nx = n_row // CORES
    x, core = row // CORES, row % CORES
    z, y = col // NY, col % NY
    yp = z * NY + (1 - y)
    rb, cb = anc.shape[0], anc.shape[1]
    kr, cs = low.shape[0], low.shape[1]
    side = low.shape[2]
    rows = upp.shape[1]
    rs = rows // side
    ny = rows - nq
    yf = nyp * py
    partner = x * CORES + (1 - core)

    def remote(src, dst, ss, rsem, **where):
        return pltpu.make_async_remote_copy(
            src_ref=src, dst_ref=dst, send_sem=ss, recv_sem=rsem, device_id=where
        )

    ca = pltpu.make_async_copy(anc, a, loc.at[0])
    cl = pltpu.make_async_copy(low, lbuf.at[pl.ds(row * kr, kr)], loc.at[1])
    cu = pltpu.make_async_copy(upp.at[0], ubuf.at[col], loc.at[2])
    cp = pltpu.make_async_copy(piv_in.at[0], piv, loc.at[3])
    cm = pltpu.make_async_copy(mem_in, mem, loc.at[4])
    cm.start()
    cu.start()
    cl.start()
    ca.start()
    cp.start()

    bar = pltpu.get_barrier_semaphore()
    for dx in range(1, n_row):
        pl.semaphore_signal(bar, inc=1, device_id={"row": (row + dx) % n_row})
    pl.semaphore_signal(bar, inc=1, device_id={"col": yp})

    @pl.when(z > 0)
    def _():
        pl.semaphore_signal(bar, inc=1, device_id={"col": col - NY})

    @pl.when(z < nz - 1)
    def _():
        pl.semaphore_signal(bar, inc=1, device_id={"col": col + NY})

    peers = n_row + jnp.where(z > 0, 1, 0) + jnp.where(z < nz - 1, 1, 0)
    pl.semaphore_wait(bar, peers)

    L_S, UA_S, UY_S, RY_S, RH_S, RZ_S, RQ_S, PR_S, PU_S, D_S, UZ_S = range(11)

    def l_own(r2):
        blk = lbuf.at[pl.ds(row * kr, kr)]
        return remote(blk, blk, sent.at[L_S], l_r.at[row], row=r2)

    def l_recv(r2):
        blk = lbuf.at[pl.ds(r2 * kr, kr)]
        return remote(blk, blk, sent.at[L_S], l_r.at[r2], row=partner)

    def uy(k, late, rsem):
        part = pl.ds(0, ny) if late else pl.ds(ny, nq)
        blk = ubuf.at[k, part]
        return remote(blk, blk, sent.at[UY_S if late else UA_S], uy_r.at[rsem], col=yp)

    def uy_own(kind):
        return uy(col, kind == 1, z if kind else nz)

    def uy_got(kind, zs):
        return uy(zs * NY + (1 - y), kind == 1, zs if kind else nz)

    def uy_pass(zs):
        return uy(zs * NY + y, True, zs)

    def uz(zs, kind, up):
        k = zs * NY + (1 - y if kind == 2 else y)
        blk = ubuf.at[k, pl.ds(0, ny) if kind == 0 else pl.ds(ny, nq)]
        to = col + NY if up else col - NY
        return remote(blk, blk, sent.at[UZ_S + kind], uz_r.at[zs, kind], col=to)

    half = side // 2
    nh = nyp // 2

    def ypart(h):
        return (
            pl.ds(pl.multiple_of((h % nh) * (2 * py), 16), 2 * py),
            pl.ds(pl.multiple_of((h // nh) * half, half), half),
        )

    def zrows(f, base=yf):
        return pl.ds(pl.multiple_of(base + f * pz, 16), pz)

    def ry(zd, h):
        part = ypart(h)
        return remote(
            pl_buf.at[zd * NY + (1 - y), *part], yr.at[zd, *part], sent.at[RY_S],
            ry_r.at[zd, h], col=yp,
        )

    def rh(f):
        part = zrows(f)
        return remote(pl_buf.at[yp, part], yr.at[z, part], sent.at[RH_S], rh_r.at[f], col=yp)

    def rz(zd, h, up):
        slot = zd + 1 if up else zd
        to = col + NY if up else col - NY
        part = ypart(h)
        return remote(
            pl_buf.at[zd * NY + y, *part], zr.at[slot, *part], sent.at[RZ_S],
            rz_r.at[slot, h], col=to,
        )

    def rf(zd, f, up):
        slot = zd + 1 if up else zd
        to = col + NY if up else col - NY
        part = zrows(f)
        return remote(
            pl_buf.at[zd * NY + y, part], zr.at[slot, part], sent.at[RZ_S],
            rf_r.at[slot, f], col=to,
        )

    def rq(zd, f, up):
        slot = zd + 1 if up else zd
        to = col + NY if up else col - NY
        return remote(
            pl_buf.at[zd * NY + (1 - y), zrows(f)], zq.at[slot, zrows(f, 0)], sent.at[RQ_S],
            rq_r.at[slot, f], col=to,
        )

    def held(k):
        return k // (kr * CORES) * kr + k % kr

    def pr_copy(k):
        slot = held(k)
        return remote(pu.at[k], pr.at[slot], sent.at[PR_S], pr_r.at[slot], row=partner)

    def pu_copy(k):
        return remote(pu.at[k], ur.at[x, k % kr], sent.at[PU_S], pu_r.at[x, k % kr], row=k // kr)

    def pu_got(x2, p):
        return remote(
            pu.at[0], ur.at[x2, p], sent.at[PU_S], pu_r.at[x2, p], row=x2 * CORES + core
        )

    def keeps(k):
        return (k // kr) % CORES == core

    def leaves(k):
        return k // (kr * CORES) != x

    def d_copy(r2, c):
        return remote(ds.at[c], dr.at[row, c], sent.at[D_S], d_r.at[row, c], row=r2)

    def d_got(r2, c):
        return remote(ds.at[c], dr.at[r2, c], sent.at[D_S], d_r.at[r2, c], row=r2)

    def d_relay(x2, c):
        r2 = x2 * CORES + core
        blk = dr.at[r2, c]
        return remote(blk, blk, sent.at[D_S], d_r.at[r2, c], row=partner)

    def each_dir(fn):
        @pl.when(z > 0)
        def _():
            fn(False)

        @pl.when(z < nz - 1)
        def _():
            fn(True)

    def row_member(k, i):
        m = mem[k, row * rs + i]
        return m >= 0, jnp.clip(m - row * rb, 0, rb - 1)

    def col_member(k, j):
        m = mem[k, col * cs + j]
        return m >= 0, jnp.clip(m - col * cb, 0, cb - 1)

    planes = nz // nx
    edge = jnp.logical_or(z == 0, z == nz - 1)

    def mine(zs):
        return zs // planes == x

    def last_to(up):
        e = nz - 1 if up else 0
        return jnp.where(mine(e), nz - 2 if up else 1, nz - 1 - e)

    def held_back(zs, up):
        return jnp.logical_and(z == (nz - 2 if up else 1), zs == last_to(up))

    def order(i):
        near_half = jnp.where(i % 2 == 0, nz // 2 + i // 2, i // 2)
        dist = jnp.where(mine(z), near_half, i)
        inner_low = jnp.where(i < nz // 2, nz // 2 + i, nz - 1 - i)
        inner_high = jnp.where(i < nz // 2, nz // 2 - 1 - i, i)
        return jnp.where(
            edge, jnp.where(z == 0, dist, nz - 1 - dist),
            jnp.where(2 * x < nx, inner_low, inner_high),
        )

    zero = jnp.zeros((), BF)

    def block(i):
        return pl.ds(pl.multiple_of(i * side, side), side)

    def lower_part(k):
        cols = [col_member(k, j) for j in range(cs)]
        panels = [jnp.where(cols[j][0], lbuf[k, j], zero) for j in range(cs)]

        def one(i, _):
            ok, ri = row_member(k, i)
            tot = None
            for j in range(cs):
                t = jnp.dot(a[ri, cols[j][1]], panels[j], preferred_element_type=F32)
                tot = t if tot is None else tot + t
            pl_buf[k, block(i)] = jnp.where(ok, tot, 0.0).astype(BF)
            return 0

        lax.fori_loop(0, rs, one, 0)

    def upper_part(k):
        mem_rows = [row_member(k, i) for i in range(rs)]

        def one(j, _):
            ok, cj = col_member(k, j)
            tot = None
            for i in range(rs):
                t = jnp.dot(
                    jnp.where(mem_rows[i][0], ubuf[k, block(i)], zero), a[mem_rows[i][1], cj],
                    preferred_element_type=F32,
                )
                tot = t if tot is None else tot + t
            pu[k, j] = jnp.where(ok, tot, 0.0).astype(BF)
            return 0

        lax.fori_loop(0, cs, one, 0)

        @pl.when(jnp.logical_not(keeps(k)))
        def _():
            pr_copy(k).start()

    def finish(k):
        @pl.when(jnp.logical_and(keeps(k), leaves(k)))
        def _():
            pr_copy(k).wait_recv()
            for j in range(cs):
                pu[k, j] = (pu[k, j].astype(F32) + pr[held(k), j].astype(F32)).astype(BF)
            pu_copy(k).start()

    def lower_group(r2):
        def one(p, _):
            k = r2 * kr + (p + 1 - y) % NY
            lower_part(k)

            @pl.when(k % NY != y)
            def _():
                for h in range(nyp):
                    ry(k // NY, h).start()

            return 0

        lax.fori_loop(0, kr, one, 0)

    def both_groups(x2):
        def one(q, _):
            lower_group(x2 * CORES + jnp.where(2 * x2 >= nx, CORES - 1 - q, q))
            return 0

        lax.fori_loop(0, CORES, one, 0)

    cu.wait()
    uy_own(0).start()
    each_dir(lambda up: uz(z, 0, up).start())
    each_dir(lambda up: uz(z, 1, up).start())
    cl.wait()
    l_own(partner).start()
    for dx in range(1, nx):
        l_own(((x + dx) % nx) * CORES + core).start()
    cm.wait()
    ca.wait()
    l_recv(partner).wait_recv()
    both_groups(x)

    uy_got(0, z).wait_recv()

    def share(zs, up):
        @pl.when(jnp.logical_not(held_back(zs, up)))
        def _():
            uz(zs, 2, up).start()

    each_dir(lambda up: share(z, up))
    upper_part(col)

    def others(fn):
        for dx in range(1, nx):
            fn((x + dx) % nx)

    def add_to(k, part, terms):
        tot = pl_buf[k, *part].astype(F32)
        for t in terms:
            tot = tot + t.astype(F32)
        pl_buf[k, *part] = tot.astype(BF)

    def each_way(zd, go):
        @pl.when(zd > z)
        def _():
            go(True)

        @pl.when(zd < z)
        def _():
            go(False)

    def hop_f(zd, f, own):
        k = zd * NY + (y if own else 1 - y)
        part = zrows(f)

        def go(up):
            slot = zd + 1 if up else zd
            step = (rf if own else rq)(zd, f, up)

            @pl.when((z > 0) if up else (z < nz - 1))
            def _():
                step.wait_recv()
                add_to(k, (part,), [zr[slot, part] if own else zq[slot, zrows(f, 0)]])

            step.start()

        each_way(zd, go)

    def hop_y(zd, h):
        k = zd * NY + y
        part = ypart(h)

        def go(up):
            slot = zd + 1 if up else zd
            step = rz(zd, h, up)
            ry(zd, h).wait_recv()

            @pl.when((z > 0) if up else (z < nz - 1))
            def _():
                step.wait_recv()
                add_to(k, part, [yr[zd, *part], zr[slot, *part]])

            @pl.when((z == 0) if up else (z == nz - 1))
            def _():
                add_to(k, part, [yr[zd, *part]])

            step.start()

        each_way(zd, go)

    def firsts(zds, own):
        def one(f, _):
            for zd, ok in zds:
                @pl.when(ok)
                def _():
                    hop_f(zd, f, own)

            return 0

        lax.fori_loop(0, nf, one, 0)

    def ends(j):
        return [(jnp.where(z == 0, nz - 1 - j, j), j < nz - 1)]

    def opening(early):
        def one(j, _):
            zd = ends(j)[0][0]
            firsts([(zd, mine(zd) if early else jnp.logical_not(mine(zd)))], False)
            return 0

        lax.fori_loop(0, nz - 1, one, 0)

    def relay(x2):
        l_recv(x2 * CORES + core).wait_recv()
        l_recv(x2 * CORES + core).start()

    def by_side(d, fn):
        @pl.when(z - d >= 0)
        def _():
            fn(z - d, True)

        @pl.when(z + d <= nz - 1)
        def _():
            fn(z + d, False)

    def take(kind):
        def one(zs, up):
            uz(zs, kind, up).wait_recv()

            @pl.when((z < nz - 1) if up else (z > 0))
            def _():
                if kind == 2:
                    share(zs, up)
                else:
                    uz(zs, kind, up).start()

        return one

    by_side(1, take(0))

    @pl.when(edge)
    def _():
        opening(True)

    others(relay)
    by_side(1, take(1))

    def late(x2):
        l_recv(x2 * CORES + 1 - core).wait_recv()
        both_groups(x2)

    others(late)

    @pl.when(edge)
    def _():
        opening(False)

    @pl.when(jnp.logical_not(edge))
    def _():
        by_side(1, take(2))

    def hand_on(zs):
        @pl.when(zs == z)
        def _():
            uy_own(1).start()

        @pl.when(zs != z)
        def _():
            uy_pass(zs).start()

    def sides(d, fn):
        def one(s, _):
            zs = z + (2 * s - 1) * d

            @pl.when(jnp.logical_and(zs >= 0, zs < nz))
            def _():
                fn(zs)

            return 0

        lax.fori_loop(0, 2, one, 0)

    def near(d):
        sides(d, lambda zs: upper_part(zs * NY + y))

    def near_done(d):
        sides(d, lambda zs: finish(zs * NY + y))

    def across(i):
        zs = order(i)

        @pl.when(jnp.logical_and(edge, zs > z))
        def _():
            uz(zs, 2, False).wait_recv()

        @pl.when(jnp.logical_and(edge, zs < z))
        def _():
            uz(zs, 2, True).wait_recv()

        uy_got(1, zs).wait_recv()
        upper_part(zs * NY + (1 - y))

    def across_done(i):
        finish(order(i) * NY + (1 - y))

    def home():
        def one(f, _):
            each_dir(lambda up: rq(z, f, not up).wait_recv())

            @pl.when(z > 0)
            def _():
                add_to(yp, (zrows(f),), [zq[z + 1, zrows(f, 0)]])

            @pl.when(z < nz - 1)
            def _():
                add_to(yp, (zrows(f),), [zq[z, zrows(f, 0)]])

            rh(f).start()
            return 0

        lax.fori_loop(0, nf, one, 0)

    def seconds(zds, hook=None, close=None):
        def piece(h, _):
            if hook is not None:
                hook(h)
            for zd, ok in zds:
                @pl.when(ok)
                def _():
                    hop_y(zd, h)

                if close is not None and zd is zds[0][0]:
                    @pl.when(h == nyp - 1)
                    def _():
                        close()

            return 0

        lax.fori_loop(0, nyp, piece, 0)

    near(1)
    finish(col)

    @pl.when(edge)
    def _():
        firsts(ends(0), True)
        seconds(ends(0))
        firsts(ends(1), True)

        def on(dist):
            hand_on(jnp.where(z == 0, dist, nz - 1 - dist))

        def one(d, _):
            by_side(d, take(0))

            @pl.when(jnp.logical_and(mine(z), d >= nz // 2))
            def _():
                on(d)

                @pl.when(d < nz - 1)
                def _():
                    on(d - nz // 2)

            @pl.when(jnp.logical_not(mine(z)))
            def _():
                @pl.when(d == 2)
                def _():
                    on(0)
                    on(1)

                @pl.when(d < nz - 1)
                def _():
                    on(d)

            by_side(d, take(1))
            near(d)
            near_done(d - 1)
            seconds(ends(d - 1))
            firsts(ends(d), True)
            return 0

        lax.fori_loop(2, nz, one, 0)
        across(0)
        near_done(nz - 1)
        home()
        hand_on(order(nz - 1))
        across(1)
        across_done(0)

    @pl.when(jnp.logical_not(edge))
    def _():
        low_half = 2 * z < nz
        short = jnp.where(low_half, z, nz - 1 - z)
        gap = nz - 1 - 2 * short
        spot = nyp - 2

        def both(s):
            s2 = s - gap
            return [
                (
                    jnp.where(low_half, s2, nz - 1 - s2),
                    jnp.logical_and(s2 >= 0, s2 < short),
                ),
                (jnp.where(low_half, nz - 1 - s, s), s >= 0),
            ]

        def others_long(s, _):
            firsts(both(s)[1:], False)
            return 0

        def others_short(s, _):
            firsts(both(s)[:1], False)
            return 0

        def one(d, _):
            by_side(d, take(0))
            by_side(d, take(1))

            @pl.when(d == nz - 2)
            def _():
                lax.fori_loop(0, nz - 1 - short, others_long, 0)

            by_side(d, take(2))
            near(d)
            near_done(d - 1)
            return 0

        lax.fori_loop(2, nz - 1, one, 0)
        for i in range(nz - 1):
            hand_on(order(i))
        def pair(s, _):
            s2 = s - gap

            def hook(h):
                now = s == nz - 2 - short

                @pl.when(jnp.logical_and(now, h - spot == 0))
                def _():
                    near_done(nz - 2)
                    across(0)

                @pl.when(jnp.logical_and(now, h - spot == 1))
                def _():
                    across(1)

            def close():
                @pl.when(s2 == short - 1)
                def _():
                    @pl.when(z == 1)
                    def _():
                        uz(last_to(False), 2, False).start()

                    @pl.when(z == nz - 2)
                    def _():
                        uz(last_to(True), 2, True).start()

            firsts(both(s), True)

            @pl.when(s == 0)
            def _():
                lax.fori_loop(0, nz - 1 - short, others_short, 0)

            seconds(both(s), hook, close)

            @pl.when(s == 0)
            def _():
                home()
                hand_on(order(nz - 1))

            return 0

        lax.fori_loop(0, nz - 1 - short, pair, 0)
        across_done(0)

    across_done(1)

    def rest(i, _):
        across(i)

        @pl.when(i > 2)
        def _():
            across_done(i - 1)

        return 0

    lax.fori_loop(2, nz - 1, rest, 0)

    def final(part, got, step):
        got.wait_recv()
        acc[*part] = pl_buf[col, *part].astype(F32) + yr[z, *part].astype(F32)

        @pl.when(z > 0)
        def _():
            step(True).wait_recv()
            acc[*part] = acc[*part] + zr[z + 1, *part].astype(F32)

        @pl.when(z < nz - 1)
        def _():
            step(False).wait_recv()
            acc[*part] = acc[*part] + zr[z, *part].astype(F32)

        low_out[0, *part] = (-acc[*part]).astype(BF)

    def final_f(f, _):
        final((zrows(f),), rh(f), lambda up: rf(z, f, up))
        return 0

    def final_y(h, _):
        final(ypart(h), ry(z, h), lambda up: rz(z, h, up))
        return 0

    lax.fori_loop(0, nf, final_f, 0)

    def side_sum(c, _):
        lax.fori_loop(c * nh, (c + 1) * nh, final_y, 0)
        cols = pl.ds(pl.multiple_of(c * half, half), half)
        tot = None
        for i in range(rs):
            t = jnp.dot(
                jnp.where(row_member(col, i)[0], ubuf[col, block(i)], zero),
                low_out[0, block(i), cols],
                preferred_element_type=F32,
            )
            tot = t if tot is None else tot + t
        dacc[c] = tot
        ds[c] = tot.astype(BF)
        others(lambda x2: d_copy(x2 * CORES + core, c).start())
        d_copy(partner, c).start()
        return 0

    lax.fori_loop(0, 2, side_sum, 0)

    across_done(nz - 2)

    def d_pass(x2):
        for c in range(2):
            d_got(x2 * CORES + core, c).wait_recv()
            d_relay(x2, c).start()

    @pl.when(edge)
    def _():
        others(d_pass)

    across(nz - 1)
    across_done(nz - 1)

    @pl.when(jnp.logical_not(edge))
    def _():
        others(d_pass)

    def piece(p, j):
        return block(p * cs + j)

    for p in range(kr):
        pr_copy(row * kr + p).wait_recv()
        for j in range(cs):
            acc[piece(p, j)] = (
                pu[row * kr + p, j].astype(F32) + pr[held(row * kr + p), j].astype(F32)
            )

    def pu_add(x2):
        for p in range(kr):
            pu_got(x2, p).wait_recv()
            for j in range(cs):
                acc[piece(p, j)] = acc[piece(p, j)] + ur[x2, p, j].astype(F32)

    others(pu_add)
    for p in range(kr):
        for j in range(cs):
            upp_out[p, j] = (-acc[piece(p, j)]).astype(BF)

    def all_sent(ref, which):
        pltpu.make_async_copy(ref, ref, sent.at[which]).wait()

    for kind in range(3):
        n = nq if kind else ny

        @pl.when(edge)
        def _():
            all_sent(ubuf.at[pl.ds(0, 1), pl.ds(0, n)], UZ_S + kind)

        @pl.when(jnp.logical_not(edge))
        def _():
            all_sent(ubuf.at[pl.ds(0, nz + 1), pl.ds(0, n)], UZ_S + kind)

    all_sent(lbuf.at[pl.ds(0, kr * (2 * nx - 1))], L_S)
    all_sent(ubuf.at[pl.ds(0, 1), pl.ds(0, nq)], UA_S)
    all_sent(ubuf.at[pl.ds(0, nz), pl.ds(0, ny)], UY_S)
    all_sent(pl_buf.at[pl.ds(0, nz), pl.ds(0, yf)], RY_S)
    all_sent(pl_buf.at[pl.ds(0, 1), pl.ds(0, nf * pz)], RH_S)
    all_sent(pl_buf.at[pl.ds(0, nz - 1)], RZ_S)
    all_sent(pl_buf.at[pl.ds(0, nz - 1), pl.ds(0, nf * pz)], RQ_S)
    all_sent(pu.at[pl.ds(0, n_col // CORES)], PR_S)
    all_sent(pu.at[pl.ds(0, kr * (nx - 1))], PU_S)

    cp.wait()

    def d_sum(c, _):
        def d_add(r2):
            dacc[c] = dacc[c] + dr[r2, c].astype(F32)

        d_got(partner, c).wait_recv()
        d_add(partner)

        def d_add_chip(x2):
            d_add(x2 * CORES + core)
            d_got(x2 * CORES + 1 - core, c).wait_recv()
            d_add(x2 * CORES + 1 - core)

        others(d_add_chip)
        cols = pl.ds(pl.multiple_of(c * half, half), half)
        diag_out[0, :, cols] = piv[:, cols] - dacc[c]
        return 0

    lax.fori_loop(0, 2, d_sum, 0)
    all_sent(dr.at[pl.ds(0, 2 * nx - 1)], D_S)


def hand_over(low, upp, diag, low_to, upp_to, diag_to, sems):
    side = diag.shape[1]
    pairs = [(upp, upp_to), (diag, diag_to)]
    for h in range(low_to.shape[1]):
        pairs.append((low.at[0, pl.ds(h * side, side)], low_to.at[0, h]))
    copies = [pltpu.make_async_copy(a, b, sems.at[i]) for i, (a, b) in enumerate(pairs)]
    for c in copies:
        c.start()
    for c in copies:
        c.wait()


def body(ancestor_inv, lower_panel, upper_panel, pivot_inv, members):
    n_col = lax.axis_size("col")
    n_row = lax.axis_size("row")
    side = ancestor_inv.shape[2]
    rb, cb = ancestor_inv.shape[:2]
    kr, cs = lower_panel.shape[:2]
    per_col, rs = upper_panel.shape[:2]
    level = members.shape[0]
    nz = n_col // NY
    assert per_col == 1 and level == n_col and kr == NY and nz == n_row
    rows = rs * side
    nf, nyp = 1, 2
    pz = rows * 3 // 8
    py = (rows - nf * pz) // nyp
    nq = rows * 25 // 64
    assert nf * pz + nyp * py == rows and pz % 16 == 0 and py % 16 == 0 and nq % 16 == 0
    blk = (side, side)
    dma = pltpu.SemaphoreType.DMA
    vmem = pl.BlockSpec(memory_space=pltpu.VMEM)
    hbm = pl.BlockSpec(memory_space=pltpu.HBM)
    outs = pl.pallas_call(
        functools.partial(kernel, n_row, n_col, nq, nf, pz, nyp, py),
        out_shape=(
            pltpu.VMEM((per_col, rows, side), BF),
            pltpu.VMEM((kr, cs) + blk, BF),
            pltpu.VMEM((per_col,) + blk, F32),
        ),
        in_specs=[hbm] * 5,
        out_specs=(vmem, vmem, vmem),
        scratch_shapes=[
            pltpu.SMEM(members.shape, jnp.int32),
            pltpu.VMEM(blk, F32),
            pltpu.VMEM((rb, cb) + blk, BF),
            pltpu.VMEM((level, cs) + blk, BF),
            pltpu.VMEM((n_col, rows, side), BF),
            pltpu.VMEM((n_col, rows, side), BF),
            pltpu.VMEM((nz, rows, side), BF),
            pltpu.VMEM((nz + 1, rows, side), BF),
            pltpu.VMEM((nz + 1, nf * pz, side), BF),
            pltpu.VMEM((level, cs) + blk, BF),
            pltpu.VMEM((level // CORES, cs) + blk, BF),
            pltpu.VMEM((n_row // CORES, kr, cs) + blk, BF),
            pltpu.VMEM((2, side, side // 2), BF),
            pltpu.VMEM((n_row, 2, side, side // 2), BF),
            pltpu.VMEM((max(rs, kr * cs) * side, side), F32),
            pltpu.VMEM((2, side, side // 2), F32),
            dma((5,)), dma((13,)), dma((n_row,)), dma((nz + 1,)), dma((nz, 3)),
            dma((nz, nyp)), dma((nf,)), dma((nz + 1, nyp)), dma((nz + 1, nf)),
            dma((nz + 1, nf)), dma((n_col // CORES,)), dma((n_row // CORES, kr)), dma((n_row, 2)),
        ],
        compiler_params=pltpu.CompilerParams(
            collective_id=0, has_side_effects=True, vmem_limit_bytes=60 * 1024 * 1024
        ),
    )(members, ancestor_inv, lower_panel, upper_panel.reshape(per_col, rows, side), pivot_inv)
    return pl.pallas_call(
        hand_over,
        out_shape=(
            jax.ShapeDtypeStruct((per_col, rs) + blk, BF),
            jax.ShapeDtypeStruct((kr, cs) + blk, BF),
            jax.ShapeDtypeStruct((per_col,) + blk, F32),
        ),
        in_specs=[vmem] * 3,
        out_specs=(hbm,) * 3,
        scratch_shapes=[dma((rs + 2,))],
    )(*(pltpu.with_memory_space_constraint(o, pltpu.VMEM) for o in outs))


def solution(mesh):
    return jax.shard_map(
        body,
        mesh=mesh,
        in_specs=(
            P("row", "col", None, None),
            P("row", "col", None, None),
            P("col", "row", None, None),
            P("col", None, None),
            P(),
        ),
        out_specs=(P("col", "row", None, None), P("row", "col", None, None), P("col", None, None)),
        check_vma=False,
    )
```

time: 75.3 us -> 74.3 us (0.987)
  no operation moved by 1% of the time
where the time goes in v4:
time: 74.3 us; the launch traced here: 73.7 us
  Pallas kernels  73.1 us (98%)
    pallas_call x1, Pallas kernels, body(): pl.pallas_call(functools.partial(kernel, n_row, n_col, nq, nf, pz, nyp, p...  72 us

profile of v4, /device:TPU:11, one launch (start us, length us, event | category | flops | bytes accessed | tf_op | source)
XLA Modules:
  0.0 73.7 jit_solution(2899129289473615801)
XLA Ops:
  0.6 72.0 %shard_map.76 = (bf16[1,1024,256]{2,1,0:T(8,128)(2,1)S(1)}, bf16[2,2,256,256]{3,2,1,0:T(8,128)(2,1)S(1)}, f32[1,256,256]{2,1,0:T(8,128)S(1)}) custom-call(s32[8,16]{1,0:T(8,128)} %mem_in.1, bf16[8,4,256,256]{3,2,1,0:T(8,128)(2,1)} %anc.1, bf16[2,2,256,256]{3,2,1,0:T(8,128)(2,1)} %low.1, bf16[1,1024,256]{2,1,0:T(8,128)(2,1)} %bitcast.1, f32[1,256,256]{2,1,0:T(8,128)} %piv_in.1), custom_call_target="tpu_custom_call" | custom-call | tf_op jit(solution)/shard_map/pallas_call | solution.py:834
  72.6 1.1 %shard_map.77 = (bf16[1,4,256,256]{3,2,1,0:T(8,128)(2,1)}, bf16[2,2,256,256]{3,2,1,0:T(8,128)(2,1)}, f32[1,256,256]{2,1,0:T(8,128)}) custom-call(bf16[1,1024,256]{2,1,0:T(8,128)(2,1)S(1)} %get-tuple-element.6.low, bf16[2,2,256,256]{3,2,1,0:T(8,128)(2,1)S(1)} %get-tuple-element.7.upp, f32[1,256,256]{2,1,0:T(8,128)S(1)} %get-tuple-element.8.diag), custom_call_target="tpu_custom_call" | custom-call | tf_op jit(solution)/shard_map/pallas_call | solution.py:868

commit v5 on v4

--- a/solution.py
+++ b/solution.py
@@ -47,11 +47,6 @@
     cu = pltpu.make_async_copy(upp.at[0], ubuf.at[col], loc.at[2])
     cp = pltpu.make_async_copy(piv_in.at[0], piv, loc.at[3])
     cm = pltpu.make_async_copy(mem_in, mem, loc.at[4])
-    cm.start()
-    cu.start()
-    cl.start()
-    ca.start()
-    cp.start()
 
     bar = pltpu.get_barrier_semaphore()
     for dx in range(1, n_row):
@@ -66,6 +61,11 @@
     def _():
         pl.semaphore_signal(bar, inc=1, device_id={"col": col + NY})
 
+    cu.start()
+    cl.start()
+    ca.start()
+    cm.start()
+    cp.start()
     peers = n_row + jnp.where(z > 0, 1, 0) + jnp.where(z < nz - 1, 1, 0)
     pl.semaphore_wait(bar, peers)
 
@@ -597,6 +597,12 @@
 
         def one(d, _):
             by_side(d, take(0))
+
+            @pl.when(d == nz - 2)
+            def _():
+                for i in range(nz - 1):
+                    hand_on(order(i))
+
             by_side(d, take(1))
 
             @pl.when(d == nz - 2)
@@ -609,8 +615,6 @@
             return 0
 
         lax.fori_loop(2, nz - 1, one, 0)
-        for i in range(nz - 1):
-            hand_on(order(i))
         def pair(s, _):
             s2 = s - gap
 

time: 74.3 us -> 74.3 us (level)
  no operation moved by 1% of the time
where the time goes in v5:
time: 74.3 us; the launch traced here: 73.4 us
  Pallas kernels  72.7 us (98%)
    pallas_call x1, Pallas kernels, body(): pl.pallas_call(functools.partial(kernel, n_row, n_col, nq, nf, pz, nyp, p...  71.6 us

profile of v5, /device:TPU:11, one launch (start us, length us, event | category | flops | bytes accessed | tf_op | source)
XLA Modules:
  0.0 73.4 jit_solution(12168822278317187271)
XLA Ops:
  0.6 71.6 %shard_map.76 = (bf16[1,1024,256]{2,1,0:T(8,128)(2,1)S(1)}, bf16[2,2,256,256]{3,2,1,0:T(8,128)(2,1)S(1)}, f32[1,256,256]{2,1,0:T(8,128)S(1)}) custom-call(s32[8,16]{1,0:T(8,128)} %mem_in.1, bf16[8,4,256,256]{3,2,1,0:T(8,128)(2,1)} %anc.1, bf16[2,2,256,256]{3,2,1,0:T(8,128)(2,1)} %low.1, bf16[1,1024,256]{2,1,0:T(8,128)(2,1)} %bitcast.1, f32[1,256,256]{2,1,0:T(8,128)} %piv_in.1), custom_call_target="tpu_custom_call" | custom-call | tf_op jit(solution)/shard_map/pallas_call | solution.py:838
  72.3 1.1 %shard_map.77 = (bf16[1,4,256,256]{3,2,1,0:T(8,128)(2,1)}, bf16[2,2,256,256]{3,2,1,0:T(8,128)(2,1)}, f32[1,256,256]{2,1,0:T(8,128)}) custom-call(bf16[1,1024,256]{2,1,0:T(8,128)(2,1)S(1)} %get-tuple-element.6.low, bf16[2,2,256,256]{3,2,1,0:T(8,128)(2,1)S(1)} %get-tuple-element.7.upp, f32[1,256,256]{2,1,0:T(8,128)S(1)} %get-tuple-element.8.diag), custom_call_target="tpu_custom_call" | custom-call | tf_op jit(solution)/shard_map/pallas_call | solution.py:872

commit v6 on v5

--- a/solution.py
+++ b/solution.py
@@ -97,7 +97,7 @@
         k = zs * NY + (1 - y if kind == 2 else y)
         blk = ubuf.at[k, pl.ds(0, ny) if kind == 0 else pl.ds(ny, nq)]
         to = col + NY if up else col - NY
-        return remote(blk, blk, sent.at[UZ_S + kind], uz_r.at[zs, kind], col=to)
+        return remote(blk, blk, sent.at[UZ_S + kind], uz_r.at[zs if up else zs - 1, kind], col=to)
 
     half = side // 2
     nh = nyp // 2
@@ -156,12 +156,7 @@
         return remote(pu.at[k], pr.at[slot], sent.at[PR_S], pr_r.at[slot], row=partner)
 
     def pu_copy(k):
-        return remote(pu.at[k], ur.at[x, k % kr], sent.at[PU_S], pu_r.at[x, k % kr], row=k // kr)
-
-    def pu_got(x2, p):
-        return remote(
-            pu.at[0], ur.at[x2, p], sent.at[PU_S], pu_r.at[x2, p], row=x2 * CORES + core
-        )
+        return remote(pu.at[k], ur.at[x, k % kr], sent.at[PU_S], pu_r.at[0], row=k // kr)
 
     def keeps(k):
         return (k // kr) % CORES == core
@@ -747,10 +742,11 @@
 
     def pu_add(x2):
         for p in range(kr):
-            pu_got(x2, p).wait_recv()
             for j in range(cs):
                 acc[piece(p, j)] = acc[piece(p, j)] + ur[x2, p, j].astype(F32)
 
+    some = ur.at[pl.ds(0, nx - 1)]
+    pltpu.make_async_copy(some, some, pu_r.at[0]).wait()
     others(pu_add)
     for p in range(kr):
         for j in range(cs):
@@ -829,7 +825,7 @@
     nf, nyp = 1, 2
     pz = rows * 3 // 8
     py = (rows - nf * pz) // nyp
-    nq = rows * 25 // 64
+    nq = rows * 13 // 32
     assert nf * pz + nyp * py == rows and pz % 16 == 0 and py % 16 == 0 and nq % 16 == 0
     blk = (side, side)
     dma = pltpu.SemaphoreType.DMA
@@ -861,9 +857,9 @@
             pltpu.VMEM((n_row, 2, side, side // 2), BF),
             pltpu.VMEM((max(rs, kr * cs) * side, side), F32),
             pltpu.VMEM((2, side, side // 2), F32),
-            dma((5,)), dma((13,)), dma((n_row,)), dma((nz + 1,)), dma((nz, 3)),
+            dma((5,)), dma((13,)), dma((n_row,)), dma((nz + 1,)), dma((nz - 1, 3)),
             dma((nz, nyp)), dma((nf,)), dma((nz + 1, nyp)), dma((nz + 1, nf)),
-            dma((nz + 1, nf)), dma((n_col // CORES,)), dma((n_row // CORES, kr)), dma((n_row, 2)),
+            dma((nz + 1, nf)), dma((n_col // CORES,)), dma((1,)), dma((n_row, 2)),
         ],
         compiler_params=pltpu.CompilerParams(
             collective_id=0, has_side_effects=True, vmem_limit_bytes=60 * 1024 * 1024

time: 74.3 us -> 74.3 us (level)
  no operation moved by 1% of the time
where the time goes in v6:
time: 74.3 us; the launch traced here: 73.7 us
  Pallas kernels  73 us (98%)
    pallas_call x1, Pallas kernels, body(): pl.pallas_call(functools.partial(kernel, n_row, n_col, nq, nf, pz, nyp, p...  71.9 us

profile of v6, /device:TPU:11, one launch (start us, length us, event | category | flops | bytes accessed | tf_op | source)
XLA Modules:
  0.0 73.7 jit_solution(16450563497085510008)
XLA Ops:
  0.6 71.9 %shard_map.76 = (bf16[1,1024,256]{2,1,0:T(8,128)(2,1)S(1)}, bf16[2,2,256,256]{3,2,1,0:T(8,128)(2,1)S(1)}, f32[1,256,256]{2,1,0:T(8,128)S(1)}) custom-call(s32[8,16]{1,0:T(8,128)} %mem_in.1, bf16[8,4,256,256]{3,2,1,0:T(8,128)(2,1)} %anc.1, bf16[2,2,256,256]{3,2,1,0:T(8,128)(2,1)} %low.1, bf16[1,1024,256]{2,1,0:T(8,128)(2,1)} %bitcast.1, f32[1,256,256]{2,1,0:T(8,128)} %piv_in.1), custom_call_target="tpu_custom_call" | custom-call | tf_op jit(solution)/shard_map/pallas_call | solution.py:834
  72.6 1.1 %shard_map.77 = (bf16[1,4,256,256]{3,2,1,0:T(8,128)(2,1)}, bf16[2,2,256,256]{3,2,1,0:T(8,128)(2,1)}, f32[1,256,256]{2,1,0:T(8,128)}) custom-call(bf16[1,1024,256]{2,1,0:T(8,128)(2,1)S(1)} %get-tuple-element.6.low, bf16[2,2,256,256]{3,2,1,0:T(8,128)(2,1)S(1)} %get-tuple-element.7.upp, f32[1,256,256]{2,1,0:T(8,128)S(1)} %get-tuple-element.8.diag), custom_call_target="tpu_custom_call" | custom-call | tf_op jit(solution)/shard_map/pallas_call | solution.py:868
